TPU v7x, 128 devices: a whole 4x4x4 slice. The times are simulated.
128 devices in a mesh: data: 1, store: 2 (over core), model: 64 (over z, y, x).
Axes of the slice: x: 4, y: 4, z: 4, core: 2. Of those that a mesh axis runs over, the one named last changes fastest.
Arguments:
- queries: bfloat16 [16, 2560], P('data')
- w_head: bfloat16 [2560, 51200], P(None, 'model')
- store_keys: bfloat16 [262144, 2560], P(('store', 'model'))
- store_tok: int32 [262144], P(('store', 'model'))
- temperature: float32 [], replicated
- mix_weight: float32 [], replicated
Outputs:
- output: float32 [16, 51200], P(('data', 'store'), 'model')
All inputs are finite; a program needn't handle non-finite values.
Results may differ from a plain program's by a relative error of at most 0.001.
Values are sent between devices in bfloat16 or wider.
A program may use at most 1 GiB of HBM per device.

v0:
```python
import jax
import jax.numpy as jnp
from jax import lax
from jax.sharding import PartitionSpec as P


def solution(mesh):
    store_devs = mesh.shape["store"]
    model_devs = mesh.shape["model"]
    group_axes = ("store", "model")

    def local_step(queries, w_head, store_keys, store_tok, value_a11, mix_weight):
        vocab_loc = w_head.shape[1]
        rows_loc = queries.shape[0] // store_devs
        key_dots = lax.dot_general(store_keys, queries, (((1,), (1,)), ((), ())), preferred_element_type=jnp.float32)
        key_norms = jnp.sum(jnp.square(store_keys.astype(jnp.float32)), axis=1)
        scores = (2.0 * key_dots - key_norms[:, None]) / value_a11
        row_top = lax.pmax(jnp.max(scores, axis=0), group_axes)
        weights = jnp.exp(scores - row_top)
        row_total = lax.psum(jnp.sum(weights, axis=0), group_axes)
        histogram = jax.ops.segment_sum(weights, store_tok, num_segments=vocab_loc * model_devs)
        histogram = lax.psum_scatter(histogram, "model", scatter_dimension=0, tiled=True)
        histogram = lax.psum_scatter(histogram, "store", scatter_dimension=1, tiled=True)
        row_start = lax.axis_index("store") * rows_loc
        my_rows = lax.dynamic_slice_in_dim(queries, row_start, rows_loc, axis=0)
        my_total = lax.dynamic_slice_in_dim(row_total, row_start, rows_loc)
        logits = lax.dot_general(w_head, my_rows, (((0,), (1,)), ((), ())), preferred_element_type=jnp.float32)
        lm_top = lax.pmax(jnp.max(logits, axis=0), "model")
        lm_exp = jnp.exp(logits - lm_top)
        lm_total = lax.psum(jnp.sum(lm_exp, axis=0), "model")
        mixed = mix_weight * (histogram / my_total) + (1.0 - mix_weight) * (lm_exp / lm_total)
        return jnp.log(mixed).T

    return jax.shard_map(local_step, mesh=mesh, in_specs=(P("data", None), P(None, "model"), P(group_axes, None), P(group_axes), P(), P()), out_specs=P(("data", "store"), "model"), check_vma=False)
```

profile of v0, /device:TPU:1, one launch (start us, length us, event | category | flops | bytes accessed | tf_op | source)
XLA Modules:
  0.0 548.0 jit_solution(5524370640236171491)
XLA Ops:
  6.5 0.0 copy-start
  6.5 0.0 reduce-scatter.4.cloned.1.call-start
  7.2 0.0 copy-start.1
  7.2 6.2 %multiply_reduce_fusion = f32[2048]{0:T(1024)S(1)} fusion(bf16[2048,2560]{1,0:T(8,128)(2,1)} %param.8), kind=kLoop, calls=%fused_computation.1 | loop fusion | flops 15726592 | bytes 10493952 | tf_op jit(solution)/shard_map/reduce_sum | solution.py:16
  13.5 0.0 copy-done
  13.5 0.7 copy-done.1
  14.2 2.9 fusion.13
  17.1 68.7 %pmax.14 = f32[16]{0:T(128)S(1)} all-reduce(f32[16]{0:T(128)S(1)} %get-tuple-element.7), channel_id=1, replica_groups=mesh['data'=1,'store'=2,'model'=64] {'store','model'}, use_global_device_ids=true, to_apply=%region_2.0 | all-reduce | flops 16 | bytes 128 | tf_op jit(solution)/shard_map/pmax | solution.py:18
  85.8 0.2 fusion.12
  86.0 0.3 copy.9
  86.4 21.9 %scatter_custom_fusion = f32[51200,16]{1,0:T(8,128)} fusion(s32[2048]{0:T(1024)} %param.9, f32[2048,16]{1,0:T(8,128)S(1)} %copy.9, f32[]{:T(128)} %constant.9.clone.1), kind=kCustom, calls=%fused_computation.2 | custom fusion | flops 32768 | bytes 3277312 | tf_op jit(solution)/shard_map/scatter-add | solution.py:21
  108.2 0.0 copy-start.2
  108.2 0.0 reduce-scatter.4.cloned.1.call-update
  108.3 3.5 fusion.14
  111.7 156.5 %pmax.15 = f32[8]{0:T(128)S(1)} all-reduce(f32[8]{0:T(128)S(1)} %get-tuple-element.9), channel_id=1, replica_groups=mesh['data'=1,'store'=2,'model'=64] {'model'}, use_global_device_ids=true, to_apply=%region_9.0 | all-reduce | flops 8 | bytes 64 | tf_op jit(solution)/shard_map/pmax | solution.py:28
  268.2 0.2 fusion.10
  268.4 90.2 %psum.14 = f32[16]{0:T(128)S(1)} all-reduce(f32[16]{0:T(128)S(1)} %get-tuple-element.5), channel_id=1, replica_groups=mesh['data'=1,'store'=2,'model'=64] {'store','model'}, use_global_device_ids=true, to_apply=%region_7.0 | all-reduce | flops 16 | bytes 128 | tf_op jit(solution)/shard_map/psum | solution.py:20
  358.6 154.4 %psum.15 = f32[8]{0:T(128)S(1)} all-reduce(f32[8]{0:T(128)S(1)} %fusion.10), channel_id=1, replica_groups=mesh['data'=1,'store'=2,'model'=64] {'model'}, use_global_device_ids=true, to_apply=%region_11.0 | all-reduce | flops 8 | bytes 64 | tf_op jit(solution)/shard_map/psum | solution.py:30
  513.7 0.1 dynamic_slice.6
  513.7 0.0 copy-done.2
  513.7 0.6 dynamic-slice
  515.0 0.0 reduce-scatter.4.cloned.1.call-done
  515.0 1.1 copy.12
  516.1 24.3 %all-reduce = f32[800,16]{0,1:T(8,128)S(1)} all-reduce(f32[800,16]{0,1:T(8,128)S(1)} %copy.12), channel_id=3, replica_groups=mesh['data'=1,'store'=2,'model'=64] {'store'}, use_global_device_ids=true, to_apply=%region_5.0.clone | all-reduce | flops 12800 | bytes 102400
  540.4 0.7 fusion.9
Async XLA Ops:
  6.5 6.9 %copy-start = (bf16[16,2560]{1,0:T(8,128)(2,1)S(1)}, bf16[16,2560]{1,0:T(8,128)(2,1)}, u32[]{:S(2)}) copy-start(bf16[16,2560]{1,0:T(8,128)(2,1)} %param.6) | copy-start | bytes 245764
  6.5 508.5 %reduce-scatter.4.cloned.1.call-start = ((), (), s32[]{:S(2)}) async-start(), calls=%async_computation.1 | async-start | bytes 26624000
  7.2 7.0 %copy-start.1 = (bf16[2048,2560]{1,0:T(8,128)(2,1)S(1)}, bf16[2048,2560]{1,0:T(8,128)(2,1)}, u32[]{:S(2)}) copy-start(bf16[2048,2560]{1,0:T(8,128)(2,1)} %param.8) | copy-start | bytes 31457284
  108.2 405.5 %copy-start.2 = (u32[128]{0:T(128)S(1)}, u32[128]{0:T(128)}, u32[]{:S(2)}) copy-start(u32[128]{0:T(128)} %constant.24) | copy-start | bytes 1540
Sparse Core Ops, SparseCore 0:
  108.4 381.5 reduce-scatter.3
where the time goes:
time: 549 us; the launch traced here: 548 us
  blocking collectives  494 us (90%)
  other arithmetic  29.2 us (5%)
  between operations  15.4 us (3%)
  matrix products  6.38 us (1%)
    pmax x1, blocking collectives, local_step(): lm_top = lax.pmax(jnp.max(logits, axis=0), 'model')  156 us
    psum x1, blocking collectives, local_step(): lm_total = lax.psum(jnp.sum(lm_exp, axis=0), 'model')  154 us
    psum x1, blocking collectives, local_step(): row_total = lax.psum(jnp.sum(weights, axis=0), group_axes)  90.2 us
    pmax x1, blocking collectives, local_step(): row_top = lax.pmax(jnp.max(scores, axis=0), group_axes)  68.7 us
    unnamed x1, blocking collectives  24.3 us
    scatter-add x1, other arithmetic, local_step(): jax.ops.segment_sum(weights, store_tok, num_segments=vocab_loc * model_devs)  21.9 us
  transfers between devices with their start and end apart: 1, of which 0 were waited for; matrix products, arithmetic and copies ran while one was open for 1% of the time, Pallas kernels for 0%

commit v1 on v0

v1 whole, which is shorter than its diff:
```python
import functools

import jax
import jax.numpy as jnp
from jax import lax
from jax.experimental import pallas as pl
from jax.experimental.pallas import tpu as pltpu
from jax.sharding import PartitionSpec as P

F32 = jnp.float32
LANES = 128
RING = 4
CHIPS = RING**3
ROWS = 8
GROUPS = LANES // ROWS
SLOTS = 18
PARTS = 3
BLOCK = SLOTS * CHIPS // RING
MSG = BLOCK + 8
BLOCK2 = BLOCK // RING
MSG2 = BLOCK2 + 8
MSG3 = 24
NBUF = 4
HROWS = 2 * SLOTS * CHIPS * PARTS
MESH = pl.DeviceIdType.MESH


def fit(cond, a, b):
    return jnp.where(cond, a, b)


def local_kernel(tau_ref, idx_ref, grp_ref, q_ref, k_ref, out_ref, qrep, sc, wx, top, *hist):
    step = pl.program_id(0)
    steps = pl.num_programs(0)
    kb = k_ref.shape[0]
    n_keys = sc.shape[0]

    @pl.when(step == 0)
    def _():
        for h in range(2):
            half = q_ref[h * ROWS : (h + 1) * ROWS, :].astype(F32)
            pair = jnp.concatenate([half, half], axis=0).astype(jnp.bfloat16)
            for g in range(GROUPS // 2):
                qrep[pl.ds(h * LANES + g * 2 * ROWS, 2 * ROWS), :] = pair
        top[...] = jnp.full(top.shape, -jnp.inf, F32)

    zero_rows = HROWS * NBUF // steps // NBUF
    span = 288

    @pl.loop(0, zero_rows // span)
    def _(i):
        for buf in hist:
            buf[pl.ds(pl.multiple_of(step * zero_rows + i * span, 8), span), :] = jnp.zeros((span, LANES), F32)

    keys = k_ref[...]
    dots = lax.dot_general(keys, qrep[...], (((1,), (1,)), ((), ())), preferred_element_type=F32)
    kf = keys.astype(F32)
    norms = jnp.sum(kf * kf, axis=1, keepdims=True)
    scores = (2.0 * dots - norms) / tau_ref[0, 0]
    sc[pl.ds(pl.multiple_of(step * kb, kb), kb), :] = scores
    top[...] = jnp.maximum(top[...], jnp.max(scores.reshape(kb // 8, 8, 2 * LANES), axis=0))

    @pl.when(step == steps - 1)
    def _():
        m = jnp.max(top[...], axis=0, keepdims=True)
        lane_group = (lax.broadcasted_iota(jnp.int32, (LANES, LANES), 1) // ROWS).astype(F32)

        def expand(c, z):
            s = sc[pl.ds(pl.multiple_of(c * LANES, LANES), LANES), :]
            w = jnp.exp(s - m)
            mine = jnp.broadcast_to(grp_ref[pl.ds(c, 1), :], (LANES, LANES)).T == lane_group
            for h in range(2):
                wx[pl.ds(c * 2 * LANES + h, LANES, stride=2), :] = jnp.where(mine, w[:, h * LANES : (h + 1) * LANES], 0.0)
            return z + jnp.sum(w.reshape(LANES // 8, 8, 2 * LANES), axis=0)

        z = lax.fori_loop(0, n_keys // LANES, expand, jnp.zeros((8, 2 * LANES), F32))
        z = jnp.sum(z, axis=0, keepdims=True)

        unroll = 8

        @pl.loop(0, n_keys // unroll)
        def _(i):
            for u in range(0, unroll, NBUF):
                at = [pl.ds(pl.multiple_of(idx_ref[i * unroll + u + b], 2), 2) for b in range(NBUF)]
                new = [
                    hist[b][at[b], :] + wx[pl.ds(pl.multiple_of((i * unroll + u + b) * 2, 2), 2), :]
                    for b in range(NBUF)
                ]
                for b in range(NBUF):
                    hist[b][at[b], :] = new[b]

        pad = jnp.zeros((6, LANES), F32)

        @pl.loop(0, PARTS * RING)
        def _(blk):
            for h in range(2):
                for t in range(BLOCK // 8):
                    at = pl.ds(blk * 2 * BLOCK + t * 16 + h, 8, stride=2)
                    total = hist[0][at, :]
                    for b in range(1, NBUF):
                        total = total + hist[b][at, :]
                    out_ref[h, blk, t * 8 : t * 8 + 8, :] = total
                lanes = slice(h * LANES, (h + 1) * LANES)
                out_ref[h, blk, BLOCK:MSG, :] = jnp.concatenate([m[:, lanes], z[:, lanes], pad], axis=0)


def comm_kernel(
    mix_ref, hist, q_ref, w_hbm, out_ref,
    wv, logits, din, d, r1, e, r2, g3, r3, tsc, knn,
    wsem, s0, v0, s1, v1, s2, v2, s3, v3,
):
    core = lax.axis_index("store")
    chip = lax.axis_index("model")
    x, y, z = chip % RING, (chip // RING) % RING, chip // (RING * RING)
    dims = ((x, 1), (y, RING), (z, RING * RING))
    order = ((0, 1, 2), (1, 2, 0), (2, 0, 1))

    def peer(axis, delta):
        at, stride = dims[axis]
        return {"model": chip + ((at + delta) % RING - at) * stride}

    barrier = pltpu.get_barrier_semaphore()
    pl.semaphore_signal(barrier, inc=1, device_id={"store": 1 - core}, device_id_type=MESH)
    for axis in range(3):
        for delta in range(1, RING):
            pl.semaphore_signal(barrier, inc=1, device_id=peer(axis, delta), device_id_type=MESH)
    head = pltpu.make_async_copy(w_hbm, wv, wsem)
    head.start()
    pl.semaphore_wait(barrier, 10)

    sends = []

    def send(src, dst, ssem, rsem, to):
        copy = pltpu.make_async_remote_copy(src_ref=src, dst_ref=dst, send_sem=ssem, recv_sem=rsem, device_id=to, device_id_type=MESH)
        copy.start()
        sends.append(copy)
        return copy

    deltas = (2, 1, 3, 0)
    first = {}
    for delta in deltas:
        for p in range(PARTS):
            at = dims[order[p][0]][0]
            blk = p * RING + (at + delta) % RING
            n = p * RING + delta
            first[p, delta] = (blk, send(hist.at[1 - core, blk], din.at[blk], s0.at[n], v0.at[n], {"store": 1 - core}))

    head.wait()
    both = lax.dot_general(q_ref[...], wv[...], (((1,), (0,)), ((), ())), preferred_element_type=F32)
    mine = jnp.where(core == 0, both[:ROWS], both[ROWS:])
    logits[...] = mine
    lm_top = jnp.max(mine, axis=1, keepdims=True)
    lm_sum = jnp.sum(jnp.exp(mine - lm_top), axis=1, keepdims=True)
    lane = lax.broadcasted_iota(jnp.int32, (ROWS, LANES), 1)
    pair = jnp.where(lane == 0, lm_top, lm_sum)
    tsc[...] = jnp.concatenate([pair] * GROUPS, axis=0)
    pair = tsc[...].T
    lm_stats = pair[0:2, :]

    pad = jnp.zeros((4, LANES), F32)

    m_own = hist[core, 0, BLOCK : BLOCK + 1, :]
    z_own = hist[core, 0, BLOCK + 1 : BLOCK + 2, :]
    stage1 = {}
    scale = None
    for delta in deltas:
        for p in range(PARTS):
            blk, copy = first[p, delta]
            copy.wait_recv()
            if scale is None:
                m_par = din[blk, BLOCK : BLOCK + 1, :]
                m = jnp.maximum(m_own, m_par)
                a, b = jnp.exp(m_own - m), jnp.exp(m_par - m)
                zz = a * z_own + b * din[blk, BLOCK + 1 : BLOCK + 2, :]
                stats = jnp.concatenate([m, zz, lm_stats, pad], axis=0)
                scale = a, b
            a, b = scale
            d[blk, 0:BLOCK, :] = a * hist[core, blk, 0:BLOCK, :] + b * din[blk, 0:BLOCK, :]
            d[blk, BLOCK:MSG, :] = stats
            if delta:
                n = p * 3 + delta - 1
                stage1[p, delta] = send(d.at[blk], r1.at[p, delta - 1], s1.at[n], v1.at[n], peer(order[p][0], delta))

    def combine(stats):
        m = functools.reduce(jnp.maximum, [s[0:1] for s in stats])
        scales = [jnp.exp(s[0:1] - m) for s in stats]
        zz = sum(c * s[1:2] for c, s in zip(scales, stats))
        lm_m = functools.reduce(jnp.maximum, [s[2:3] for s in stats])
        lm_z = sum(jnp.exp(s[2:3] - lm_m) * s[3:4] for s in stats)
        return scales, jnp.concatenate([m, zz, lm_m, lm_z, pad], axis=0)

    stage2 = {}
    for p in range(PARTS):
        for delta in range(1, RING):
            stage1[p, delta].wait_recv()
        own = p * RING + dims[order[p][0]][0]
        scales, stats = combine([d[own, BLOCK:MSG, :]] + [r1[p, i, BLOCK:MSG, :] for i in range(3)])
        for c in range(RING):
            rows = slice(c * BLOCK2, (c + 1) * BLOCK2)
            total = scales[0] * d[own, rows, :]
            for i in range(3):
                total = total + scales[i + 1] * r1[p, i, rows, :]
            e[p, c, 0:BLOCK2, :] = total
            e[p, c, BLOCK2:MSG2, :] = stats
        for delta in deltas[:3]:
            to = (dims[order[p][1]][0] + delta) % RING
            n = p * 3 + delta - 1
            stage2[p, delta] = send(e.at[p, to], r2.at[p, delta - 1], s2.at[n], v2.at[n], peer(order[p][1], delta))

    stage3 = {}
    for p in range(PARTS):
        for delta in range(1, RING):
            stage2[p, delta].wait_recv()
        own = dims[order[p][1]][0]
        scales, stats = combine([e[p, own, BLOCK2:MSG2, :]] + [r2[p, i, BLOCK2:MSG2, :] for i in range(3)])
        for c in range(RING):
            rows = slice(c * SLOTS, (c + 1) * SLOTS)
            total = scales[0] * e[p, own, rows, :]
            for i in range(3):
                total = total + scales[i + 1] * r2[p, i, rows, :]
            g3[p, c, 0:SLOTS, :] = total
            g3[p, c, SLOTS:MSG3, :] = stats[0 : MSG3 - SLOTS]
        for delta in deltas[:3]:
            to = (dims[order[p][2]][0] + delta) % RING
            n = p * 3 + delta - 1
            stage3[p, delta] = send(g3.at[p, to], r3.at[p, delta - 1], s3.at[n], v3.at[n], peer(order[p][2], delta))

    tsc[...] = jnp.zeros(tsc.shape, F32)
    slots = logits.shape[1] // GROUPS
    for p in range(PARTS):
        for delta in range(1, RING):
            stage3[p, delta].wait_recv()
        own = dims[order[p][2]][0]
        blocks = [g3[p, own]] + [r3[p, i] for i in range(3)]
        scales, stats = combine([v[SLOTS : SLOTS + 4] for v in blocks])
        count = min(SLOTS, slots - p * SLOTS)
        total = sum(c * v[0:count] for c, v in zip(scales, blocks))
        tsc[p * SLOTS : p * SLOTS + count, :] = total / stats[1:2]
        if p == 0:
            tsc[slots : slots + 2, :] = stats[2:4]

    turned = tsc[...].T
    for g in range(GROUPS):
        knn[:, g * slots : (g + 1) * slots] = turned[g * ROWS : (g + 1) * ROWS, 0:slots]
    lm = jnp.exp(logits[...] - turned[0:ROWS, slots : slots + 1]) / turned[0:ROWS, slots + 1 : slots + 2]
    mix = mix_ref[0, 0]
    out_ref[...] = jnp.log(mix * knn[...] + (1.0 - mix) * lm)

    for copy in sends:
        copy.wait_send()


def solution(mesh):
    def local_step(queries, w_head, store_keys, store_tok, temperature, mix_weight):
        n_keys, width = store_keys.shape
        vocab_loc = w_head.shape[1]
        slots = vocab_loc // GROUPS
        kb = n_keys // 4

        chip, within = store_tok // vocab_loc, store_tok % vocab_loc
        group, slot = within // slots, within % slots
        part, row = slot // SLOTS, slot % SLOTS
        x, y, z = chip % RING, (chip // RING) % RING, chip // (RING * RING)
        first = jnp.where(part == 0, x, jnp.where(part == 1, y, z))
        second = jnp.where(part == 0, y, jnp.where(part == 1, z, x))
        third = jnp.where(part == 0, z, jnp.where(part == 1, x, y))
        place = ((part * RING + first) * RING + second) * RING + third
        index = (place * SLOTS + row) * 2
        group = group.astype(F32).reshape(n_keys // LANES, LANES)

        hist = pl.pallas_call(
            local_kernel,
            grid=(n_keys // kb,),
            out_shape=jax.ShapeDtypeStruct((2, PARTS * RING, MSG, LANES), F32),
            in_specs=[
                pl.BlockSpec(memory_space=pltpu.SMEM),
                pl.BlockSpec(memory_space=pltpu.SMEM),
                pl.BlockSpec((n_keys // LANES, LANES), lambda i: (0, 0)),
                pl.BlockSpec(queries.shape, lambda i: (0, 0)),
                pl.BlockSpec((kb, width), lambda i: (i, 0)),
            ],
            out_specs=pl.BlockSpec((2, PARTS * RING, MSG, LANES), lambda i: (0, 0, 0, 0)),
            scratch_shapes=[
                pltpu.VMEM((2 * LANES, width), jnp.bfloat16),
                pltpu.VMEM((n_keys, 2 * LANES), F32),
                pltpu.VMEM((2 * n_keys, LANES), F32),
                pltpu.VMEM((8, 2 * LANES), F32),
            ]
            + [pltpu.VMEM((HROWS, LANES), F32)] * NBUF,
            compiler_params=pltpu.CompilerParams(vmem_limit_bytes=56 * 2**20),
            name="histogram",
        )(temperature.reshape(1, 1), index, group, queries, store_keys)

        return pl.pallas_call(
            comm_kernel,
            out_shape=jax.ShapeDtypeStruct((ROWS, vocab_loc), F32),
            in_specs=[
                pl.BlockSpec(memory_space=pltpu.SMEM),
                pl.BlockSpec(memory_space=pltpu.VMEM),
                pl.BlockSpec(memory_space=pltpu.VMEM),
                pl.BlockSpec(memory_space=pl.ANY),
            ],
            out_specs=pl.BlockSpec(memory_space=pltpu.VMEM),
            scratch_shapes=[
                pltpu.VMEM(w_head.shape, jnp.bfloat16),
                pltpu.VMEM((ROWS, vocab_loc), F32),
                pltpu.VMEM((PARTS * RING, MSG, LANES), F32),
                pltpu.VMEM((PARTS * RING, MSG, LANES), F32),
                pltpu.VMEM((PARTS, RING - 1, MSG, LANES), F32),
                pltpu.VMEM((PARTS, RING, MSG2, LANES), F32),
                pltpu.VMEM((PARTS, RING - 1, MSG2, LANES), F32),
                pltpu.VMEM((PARTS, RING, MSG3, LANES), F32),
                pltpu.VMEM((PARTS, RING - 1, MSG3, LANES), F32),
                pltpu.VMEM((LANES, LANES), F32),
                pltpu.VMEM((ROWS, vocab_loc), F32),
                pltpu.SemaphoreType.DMA,
                pltpu.SemaphoreType.DMA((12,)),
                pltpu.SemaphoreType.DMA((12,)),
            ]
            + [pltpu.SemaphoreType.DMA((9,))] * 6,
            compiler_params=pltpu.CompilerParams(collective_id=0, has_side_effects=True, vmem_limit_bytes=48 * 2**20),
            name="exchange",
        )(mix_weight.reshape(1, 1), hist, queries, w_head)

    return jax.shard_map(
        local_step,
        mesh=mesh,
        in_specs=(P("data", None), P(None, "model"), P(("store", "model"), None), P(("store", "model")), P(), P()),
        out_specs=P(("data", "store"), "model"),
        check_vma=False,
    )
```

time: 549 us -> 54.2 us (0.10)
  blocking collectives: 494 us -> 0 us
  Pallas kernels: 0 us -> 41.3 us
  other arithmetic: 29.2 us -> 1.35 us
  between operations: 15.4 us -> 1.31 us
  local copies, waits for them, and re-layouts: 2.87 us -> 9.87 us
  matrix products: 6.38 us -> 0 us
    psum x2 -> x0, blocking collectives: 245 us -> none  [the longest x1 154 us: local_step(): lm_total = lax.psum(jnp.sum(lm_exp, axis=0), 'model')]
    pmax x2 -> x0, blocking collectives: 225 us -> none  [the longest x1 156 us: local_step(): lm_top = lax.pmax(jnp.max(logits, axis=0), 'model')]
    pallas_call x0 -> x2, Pallas kernels: none -> 41.3 us  [the longest x1 26.6 us: local_step(): pl.pallas_call(comm_kernel, out_shape=jax.ShapeDtypeStruct((ROWS, vocab_l...]
    unnamed x1 -> x0, blocking collectives: 24.3 us -> none
    scatter-add x1 -> x0, other arithmetic: 21.9 us -> none  [local_step(): jax.ops.segment_sum(weights, store_tok, num_segments=vocab_loc * model_devs)]
    unnamed x8 -> x6, local copies, waits for them, and re-layouts: 2.46 us -> 9.87 us
    reduce_sum x3 -> x0, other arithmetic: 6.64 us -> none  [the longest x1 6.23 us: local_step(): key_norms = jnp.sum(jnp.square(store_keys.astype(jnp.float32)), axis=1)]
    dot_general x2 -> x0, matrix products: 6.38 us -> none  [the longest x1 3.46 us: local_step(): lax.dot_general(w_head, my_rows, (((0,), (1,)), ((), ())), preferred_elem...]
  transfers between devices with their start and end apart: 1 -> 0, of which waited for: 0 -> 0; matrix products, arithmetic and copies ran while one was open for 1% -> 0% of each run, Pallas kernels for 0% -> 0%
where the time goes in v1:
time: 54.2 us; the launch traced here: 53.9 us
  Pallas kernels  41.3 us (76%)
  local copies, waits for them, and re-layouts  9.87 us (18%)
  other arithmetic  1.35 us (2%)
  between operations  1.31 us (2%)
    pallas_call x1, Pallas kernels, local_step(): pl.pallas_call(comm_kernel, out_shape=jax.ShapeDtypeStruct((ROWS, vocab_l...  26.6 us
    pallas_call x1, Pallas kernels, local_step(): pl.pallas_call(local_kernel, grid=(n_keys // kb,), out_shape=jax.ShapeDty...  14.8 us
    unnamed x6, local copies, waits for them, and re-layouts  9.87 us
    reshape x1, other arithmetic, local_step(): group = group.astype(F32).reshape(n_keys // LANES, LANES)  1.35 us

profile of v1, /device:TPU:1, one launch (start us, length us, event | category | flops | bytes accessed | tf_op | source)
XLA Modules:
  0.0 53.9 jit_solution(6552824888693864314)
XLA Ops:
  1.3 1.3 %fusion.5 = (f32[16,128]{1,0:T(8,128)}, s32[2048]{0:T(1024)}) fusion(s32[2048]{0:T(1024)} %param.9), kind=kLoop, calls=%fused_computation.22 | loop fusion | flops 192512 | bytes 24576 | tf_op jit(solution)/shard_map/reshape | solution.py:269
  2.6 14.8 %histogram.1.hist = f32[2,12,296,128]{3,2,1,0:T(8,128)} custom-call(f32[1,1]{1,0:T(1,128)} %bitcast.4.tau_ref, s32[2048]{0:T(1024)} %get-tuple-element.6.idx_ref, f32[16,128]{1,0:T(8,128)} %get-tuple-element.5.grp_ref, bf16[16,2560]{1,0:T(8,128)(2,1)} %q_ref.3, bf16[2048,2560]{1,0:T(8,128)(2,1)} %k_ref.1), custom_call_target="tpu_custom_call" | custom-call | tf_op jit(solution)/shard_map/histogram/pallas_call | solution.py:271
  17.4 0.0 copy-start.1
  17.4 7.2 %copy.7.w_hbm = bf16[2560,800]{1,0:T(8,128)(2,1)} copy(bf16[2560,800]{0,1:T(8,128)(2,1)} %param.7) | data formatting | bytes 8192000 | tf_op args[1]
  24.6 0.0 copy-done.1
  24.6 0.0 copy-start
  24.7 2.0 %copy-done = f32[2,12,296,128]{3,2,1,0:T(8,128)S(1)} copy-done((f32[2,12,296,128]{3,2,1,0:T(8,128)S(1)}, f32[2,12,296,128]{3,2,1,0:T(8,128)}, u32[]{:S(2)}) %copy-start) | copy-done | bytes 3637272
  26.7 26.6 %exchange.1 = f32[8,800]{1,0:T(8,128)S(1)} custom-call(f32[1,1]{1,0:T(1,128)} %bitcast.5.mix_ref, f32[2,12,296,128]{3,2,1,0:T(8,128)S(1)} %copy-done, bf16[16,2560]{1,0:T(8,128)(2,1)S(1)} %copy-done.1, bf16[2560,800]{1,0:T(8,128)(2,1)} %copy.7.w_hbm), custom_call_target="tpu_custom_call" | custom-call | tf_op jit(solution)/shard_map/exchange/pallas_call | solution.py:294
  53.2 0.6 %copy.11 = f32[8,800]{1,0:T(8,128)} copy(f32[8,800]{1,0:T(8,128)S(1)} %exchange.1) | data formatting | bytes 51200
Async XLA Ops:
  17.4 7.2 %copy-start.1 = (bf16[16,2560]{1,0:T(8,128)(2,1)S(1)}, bf16[16,2560]{1,0:T(8,128)(2,1)}, u32[]{:S(2)}) copy-start(bf16[16,2560]{1,0:T(8,128)(2,1)} %q_ref.3) | copy-start | bytes 245764
  24.6 2.0 %copy-start = (f32[2,12,296,128]{3,2,1,0:T(8,128)S(1)}, f32[2,12,296,128]{3,2,1,0:T(8,128)}, u32[]{:S(2)}) copy-start(f32[2,12,296,128]{3,2,1,0:T(8,128)} %histogram.1.hist) | copy-start | bytes 10911748

commit v2 on v1

--- a/solution.py
+++ b/solution.py
@@ -105,9 +105,9 @@
 
 
 def comm_kernel(
-    mix_ref, hist, q_ref, w_hbm, out_ref,
-    wv, logits, din, d, r1, e, r2, g3, r3, tsc, knn,
-    wsem, s0, v0, s1, v1, s2, v2, s3, v3,
+    mix_ref, hist, q_ref, w_ref, out_ref,
+    logits, din, d, r1, e, r2, g3, r3, tsc, knn,
+    s0, v0, s1, v1, s2, v2, s3, v3,
 ):
     core = lax.axis_index("store")
     chip = lax.axis_index("model")
@@ -124,8 +124,6 @@
     for axis in range(3):
         for delta in range(1, RING):
             pl.semaphore_signal(barrier, inc=1, device_id=peer(axis, delta), device_id_type=MESH)
-    head = pltpu.make_async_copy(w_hbm, wv, wsem)
-    head.start()
     pl.semaphore_wait(barrier, 10)
 
     sends = []
@@ -145,8 +143,7 @@
             n = p * RING + delta
             first[p, delta] = (blk, send(hist.at[1 - core, blk], din.at[blk], s0.at[n], v0.at[n], {"store": 1 - core}))
 
-    head.wait()
-    both = lax.dot_general(q_ref[...], wv[...], (((1,), (0,)), ((), ())), preferred_element_type=F32)
+    both = lax.dot_general(q_ref[...], w_ref[...], (((1,), (1,)), ((), ())), preferred_element_type=F32)
     mine = jnp.where(core == 0, both[:ROWS], both[ROWS:])
     logits[...] = mine
     lm_top = jnp.max(mine, axis=1, keepdims=True)
@@ -287,7 +284,7 @@
                 pltpu.VMEM((8, 2 * LANES), F32),
             ]
             + [pltpu.VMEM((HROWS, LANES), F32)] * NBUF,
-            compiler_params=pltpu.CompilerParams(vmem_limit_bytes=56 * 2**20),
+            compiler_params=pltpu.CompilerParams(vmem_limit_bytes=50 * 2**20),
             name="histogram",
         )(temperature.reshape(1, 1), index, group, queries, store_keys)
 
@@ -298,11 +295,10 @@
                 pl.BlockSpec(memory_space=pltpu.SMEM),
                 pl.BlockSpec(memory_space=pltpu.VMEM),
                 pl.BlockSpec(memory_space=pltpu.VMEM),
-                pl.BlockSpec(memory_space=pl.ANY),
+                pl.BlockSpec(memory_space=pltpu.VMEM),
             ],
             out_specs=pl.BlockSpec(memory_space=pltpu.VMEM),
             scratch_shapes=[
-                pltpu.VMEM(w_head.shape, jnp.bfloat16),
                 pltpu.VMEM((ROWS, vocab_loc), F32),
                 pltpu.VMEM((PARTS * RING, MSG, LANES), F32),
                 pltpu.VMEM((PARTS * RING, MSG, LANES), F32),
@@ -313,14 +309,13 @@
                 pltpu.VMEM((PARTS, RING - 1, MSG3, LANES), F32),
                 pltpu.VMEM((LANES, LANES), F32),
                 pltpu.VMEM((ROWS, vocab_loc), F32),
-                pltpu.SemaphoreType.DMA,
                 pltpu.SemaphoreType.DMA((12,)),
                 pltpu.SemaphoreType.DMA((12,)),
             ]
             + [pltpu.SemaphoreType.DMA((9,))] * 6,
-            compiler_params=pltpu.CompilerParams(collective_id=0, has_side_effects=True, vmem_limit_bytes=48 * 2**20),
+            compiler_params=pltpu.CompilerParams(collective_id=0, has_side_effects=True, vmem_limit_bytes=20 * 2**20),
             name="exchange",
-        )(mix_weight.reshape(1, 1), hist, queries, w_head)
+        )(mix_weight.reshape(1, 1), hist, queries, w_head.T)
 
     return jax.shard_map(
         local_step,

time: 54.2 us -> 43.6 us (0.80)
  local copies, waits for them, and re-layouts: 9.87 us -> 1.5 us
  Pallas kernels: 41.3 us -> 39.8 us
  other arithmetic: 1.35 us -> 0.75 us
    unnamed x6 -> x5, local copies, waits for them, and re-layouts: 9.87 us -> 1.5 us
    pallas_call x1, Pallas kernels: 14.8 us -> 13.2 us  [local_step(): pl.pallas_call(local_kernel, grid=(n_keys // kb,), out_shape=jax.ShapeDty...]
    reshape x1, other arithmetic: 1.35 us -> 0.75 us  [local_step(): group = group.astype(F32).reshape(n_keys // LANES, LANES)]
where the time goes in v2:
time: 43.6 us; the launch traced here: 43.4 us
  Pallas kernels  39.8 us (91%)
  local copies, waits for them, and re-layouts  1.5 us (3%)
  between operations  1.33 us (3%)
  other arithmetic  0.75 us (2%)
    pallas_call x1, Pallas kernels, local_step(): pl.pallas_call(comm_kernel, out_shape=jax.ShapeDtypeStruct((ROWS, vocab_l...  26.6 us
    pallas_call x1, Pallas kernels, local_step(): pl.pallas_call(local_kernel, grid=(n_keys // kb,), out_shape=jax.ShapeDty...  13.2 us
    unnamed x5, local copies, waits for them, and re-layouts  1.5 us

profile of v2, /device:TPU:1, one launch (start us, length us, event | category | flops | bytes accessed | tf_op | source)
XLA Modules:
  0.0 43.4 jit_solution(6797285419644456990)
XLA Ops:
  1.3 0.8 %fusion.5 = (f32[16,128]{1,0:T(8,128)S(1)}, s32[2048]{0:T(1024)S(1)}) fusion(s32[2048]{0:T(1024)} %param.9), kind=kLoop, calls=%fused_computation.22 | loop fusion | flops 192512 | bytes 24576 | tf_op jit(solution)/shard_map/reshape | solution.py:266
  2.0 0.0 copy-start.1
  2.1 0.9 %copy-done.1 = bf16[16,2560]{1,0:T(8,128)(2,1)S(1)} copy-done((bf16[16,2560]{1,0:T(8,128)(2,1)S(1)}, bf16[16,2560]{1,0:T(8,128)(2,1)}, u32[]{:S(2)}) %copy-start.1) | copy-done | bytes 81944
  2.9 0.0 copy-start
  2.9 13.2 %histogram.1.hist = f32[2,12,296,128]{3,2,1,0:T(8,128)S(1)} custom-call(f32[1,1]{1,0:T(1,128)} %bitcast.5.tau_ref, s32[2048]{0:T(1024)S(1)} %get-tuple-element.6.idx_ref, f32[16,128]{1,0:T(8,128)S(1)} %get-tuple-element.5.grp_ref, bf16[16,2560]{1,0:T(8,128)(2,1)S(1)} %copy-done.1, bf16[2048,2560]{1,0:T(8,128)(2,1)} %k_ref.1), custom_call_target="tpu_custom_call" | custom-call | tf_op jit(solution)/shard_map/histogram/pallas_call | solution.py:268
  16.1 0.0 copy-done
  16.1 26.6 %exchange.1 = f32[8,800]{1,0:T(8,128)S(1)} custom-call(f32[1,1]{1,0:T(1,128)} %bitcast.6.mix_ref, f32[2,12,296,128]{3,2,1,0:T(8,128)S(1)} %histogram.1.hist, bf16[16,2560]{1,0:T(8,128)(2,1)S(1)} %copy-done.1, bf16[800,2560]{1,0:T(8,128)(2,1)S(1)} %bitcast.7), custom_call_target="tpu_custom_call" | custom-call | tf_op jit(solution)/shard_map/exchange/pallas_call | solution.py:291
  42.8 0.6 %copy.10 = f32[8,800]{1,0:T(8,128)} copy(f32[8,800]{1,0:T(8,128)S(1)} %exchange.1) | data formatting | bytes 51200
Async XLA Ops:
  2.0 0.9 %copy-start.1 = (bf16[16,2560]{1,0:T(8,128)(2,1)S(1)}, bf16[16,2560]{1,0:T(8,128)(2,1)}, u32[]{:S(2)}) copy-start(bf16[16,2560]{1,0:T(8,128)(2,1)} %q_ref.3) | copy-start | bytes 245764
  2.9 13.2 %copy-start = (bf16[2560,800]{0,1:T(8,128)(2,1)S(1)}, bf16[2560,800]{0,1:T(8,128)(2,1)}, u32[]{:S(2)}) copy-start(bf16[2560,800]{0,1:T(8,128)(2,1)} %param.7) | copy-start | bytes 12288004

commit v3 on v0

v3 whole, which is shorter than its diff:
```python
import functools

import jax
import jax.numpy as jnp
from jax import lax
from jax.experimental import pallas as pl
from jax.experimental.pallas import tpu as pltpu
from jax.sharding import PartitionSpec as P

F32 = jnp.float32
LANES = 128
RING = 4
CHIPS = RING**3
ROWS = 8
GROUPS = LANES // ROWS
SLOTS = 18
PARTS = 3
BLOCK = SLOTS * CHIPS // RING
BLOCK2 = BLOCK // RING
STAT = 8
MSG = STAT + BLOCK
MSG2 = STAT + BLOCK2
MSG3 = 24
NBUF = 4
KA_LIMIT = 36
KB_LIMIT = 36
HROWS = 2 * SLOTS * CHIPS * PARTS
MESH = pl.DeviceIdType.MESH


def local_kernel(vocab_loc, tau_ref, tok_hbm, q_hbm, k_hbm, *refs):
    hist, stats_ref = refs[:NBUF], refs[NBUF]
    q_ref, k_ref, qrep, sc, wx, grp, idx, idx_smem, tok_ref, qsem, isem, tsem, ksem = refs[NBUF + 1 :]
    n_keys = k_ref.shape[0]
    quarter = n_keys // NBUF
    chunk = quarter // 2

    def fetch(j):
        rows = pl.ds(pl.multiple_of(j * chunk, chunk), chunk)
        return pltpu.make_async_copy(k_hbm.at[rows], k_ref.at[rows], ksem.at[j])

    get_tok = pltpu.make_async_copy(tok_hbm, tok_ref, tsem)
    get_tok.start()
    get_q = pltpu.make_async_copy(q_hbm, q_ref, qsem)
    get_q.start()
    for j in range(n_keys // chunk):
        fetch(j).start()

    span = 288

    @pl.loop(0, HROWS // span)
    def _(i):
        for buf in hist:
            buf[pl.ds(pl.multiple_of(i * span, 8), span), :] = jnp.zeros((span, LANES), F32)

    get_tok.wait()
    tok = tok_ref[...]
    chip, within = tok // vocab_loc, tok % vocab_loc
    slots = vocab_loc // GROUPS
    group, slot = within // slots, within % slots
    part, row = slot // SLOTS, slot % SLOTS
    x, y, z = chip % RING, (chip // RING) % RING, chip // (RING * RING)
    first = jnp.where(part == 0, x, jnp.where(part == 1, y, z))
    second = jnp.where(part == 0, y, jnp.where(part == 1, z, x))
    third = jnp.where(part == 0, z, jnp.where(part == 1, x, y))
    place = ((part * RING + first) * RING + second) * RING + third
    idx[...] = (place * SLOTS + row) * 2
    put_idx = pltpu.make_async_copy(idx, idx_smem, isem)
    put_idx.start()
    group = group.astype(F32)
    for c in range(n_keys // LANES):
        grp[c * LANES : (c + 1) * LANES, :] = jnp.broadcast_to(group[c : c + 1, :], (LANES, LANES)).T

    get_q.wait()
    for h in range(2):
        half = q_ref[h * ROWS : (h + 1) * ROWS, :].astype(F32)
        pair = jnp.concatenate([half, half], axis=0).astype(jnp.bfloat16)
        for g in range(GROUPS // 2):
            qrep[pl.ds(h * LANES + g * 2 * ROWS, 2 * ROWS), :] = pair

    tau = tau_ref[0, 0]
    lane_group = (lax.broadcasted_iota(jnp.int32, (LANES, LANES), 1) // ROWS).astype(F32)

    @pl.loop(0, NBUF)
    def _(b):
        top = jnp.full((8, 2 * LANES), -jnp.inf, F32)
        for sub in range(2):
            fetch(b * 2 + sub).wait()
            keys = k_ref[pl.ds(pl.multiple_of((b * 2 + sub) * chunk, chunk), chunk), :]
            dots = lax.dot_general(keys, qrep[...], (((1,), (1,)), ((), ())), preferred_element_type=F32)
            kf = keys.astype(F32)
            norms = jnp.sum(kf * kf, axis=1, keepdims=True)
            scores = (2.0 * dots - norms) / tau
            sc[sub * chunk : (sub + 1) * chunk, :] = scores
            top = jnp.maximum(top, jnp.max(scores.reshape(chunk // 8, 8, 2 * LANES), axis=0))
        m = jnp.max(top, axis=0, keepdims=True)
        total = jnp.zeros((8, 2 * LANES), F32)
        for c in range(quarter // LANES):
            w = jnp.exp(sc[c * LANES : (c + 1) * LANES, :] - m)
            total = total + jnp.sum(w.reshape(LANES // 8, 8, 2 * LANES), axis=0)
            at = b * quarter + c * LANES
            mine = grp[pl.ds(pl.multiple_of(at, LANES), LANES), :] == lane_group
            for h in range(2):
                wx[pl.ds(at * 2 + h, LANES, stride=2), :] = jnp.where(mine, w[:, h * LANES : (h + 1) * LANES], 0.0)
        total = jnp.sum(total, axis=0, keepdims=True)
        stats_ref[pl.ds(b, 1), :] = m
        stats_ref[pl.ds(NBUF + b, 1), :] = total

    put_idx.wait()
    unroll = 2

    @pl.loop(0, quarter // LANES)
    def _(c):
        @pl.loop(0, LANES // unroll)
        def _(i):
            for u in range(unroll):
                lane = i * unroll + u
                at = [pl.ds(pl.multiple_of(idx_smem[b * (quarter // LANES) + c, lane], 2), 2) for b in range(NBUF)]
                key = c * LANES + lane
                new = [
                    hist[b][at[b], :] + wx[pl.ds(pl.multiple_of((b * quarter + key) * 2, 2), 2), :]
                    for b in range(NBUF)
                ]
                for b in range(NBUF):
                    hist[b][at[b], :] = new[b]


def comm_kernel(
    mix_ref, h0, h1, h2, h3, kstats, q_ref, w_hbm, out_ref,
    w_ref, logits, loc, din, d, r1, e, r2, g3, r3, lt, lr, tsc, knn,
    wsem, s0, v0, s1, v1, s2, v2, s3, v3, sl, vl,
):
    core = lax.axis_index("store")
    chip = lax.axis_index("model")
    x, y, z = chip % RING, (chip // RING) % RING, chip // (RING * RING)
    dims = ((x, 1), (y, RING), (z, RING * RING))
    order = ((0, 1, 2), (1, 2, 0), (2, 0, 1))
    scope = jax.named_scope

    def peer(axis, delta):
        at, stride = dims[axis]
        return {"model": chip + ((at + delta) % RING - at) * stride}

    barrier = pltpu.get_barrier_semaphore()
    pl.semaphore_signal(barrier, inc=1, device_id={"store": 1 - core}, device_id_type=MESH)
    for axis in range(3):
        for delta in range(1, RING):
            pl.semaphore_signal(barrier, inc=1, device_id=peer(axis, delta), device_id_type=MESH)
    head = pltpu.make_async_copy(w_hbm, w_ref, wsem)
    head.start()

    hist = (h0, h1, h2, h3)
    top = functools.reduce(jnp.maximum, [kstats[b : b + 1, :] for b in range(NBUF)])
    scales = [jnp.exp(kstats[b : b + 1, :] - top) for b in range(NBUF)]
    mass = sum(c * kstats[NBUF + b : NBUF + b + 1, :] for b, c in enumerate(scales))
    half = [slice(h * LANES, (h + 1) * LANES) for h in range(2)]

    with scope("sum"):

        @pl.loop(0, PARTS * RING)
        def _(blk):
            for h in range(2):
                loc[h, blk, 0:STAT, :] = jnp.concatenate(
                    [top[:, half[h]], mass[:, half[h]], jnp.zeros((STAT - 2, LANES), F32)], axis=0
                )
                for t in range(BLOCK // 8):
                    at = pl.ds(blk * 2 * BLOCK + t * 16 + h, 8, stride=2)
                    total = scales[0][:, half[h]] * hist[0][at, :]
                    for b in range(1, NBUF):
                        total = total + scales[b][:, half[h]] * hist[b][at, :]
                    loc[h, blk, STAT + t * 8 : STAT + t * 8 + 8, :] = total

    with scope("barrier"):
        pl.semaphore_wait(barrier, 10)

    def copy(src, dst, ssem, rsem, to):
        return pltpu.make_async_remote_copy(src_ref=src, dst_ref=dst, send_sem=ssem, recv_sem=rsem, device_id=to, device_id_type=MESH)

    def span(b):
        return slice(0, MSG2) if b == 0 else slice(STAT + b * BLOCK2, STAT + (b + 1) * BLOCK2)

    def body(b):
        return slice(STAT + b * BLOCK2, STAT + (b + 1) * BLOCK2)

    near = {}
    for b in range(RING):
        for p in range(PARTS):
            blks = slice(p * RING, (p + 1) * RING)
            n = b * PARTS + p
            near[b, p] = copy(loc.at[1 - core, blks, span(b)], din.at[blks, span(b)], s0.at[n], v0.at[n], {"store": 1 - core})
            near[b, p].start()

    stage1 = {}
    for b in range(RING):
        for p in range(PARTS):
            with scope("w0"):
                near[b, p].wait_recv()
            if b == 0 and p == 0:
                m_own, m_par = loc[core, 0, 0:1, :], din[0, 0:1, :]
                m = jnp.maximum(m_own, m_par)
                c_own, c_par = jnp.exp(m_own - m), jnp.exp(m_par - m)
                zz = c_own * loc[core, 0, 1:2, :] + c_par * din[0, 1:2, :]
                stats = jnp.concatenate([m, zz, jnp.zeros((STAT - 2, LANES), F32)], axis=0)
            at = dims[order[p][0]][0]
            for delta in (2, 1, 3, 0):
                blk = p * RING + (at + delta) % RING
                if b == 0:
                    d[blk, 0:STAT, :] = stats
                d[blk, body(b), :] = c_own * loc[core, blk, body(b), :] + c_par * din[blk, body(b), :]
                if delta:
                    n = (b * PARTS + p) * 3 + delta - 1
                    stage1[b, p, delta] = copy(
                        d.at[blk, span(b)], r1.at[p, delta - 1, span(b)], s1.at[n], v1.at[n], peer(order[p][0], delta)
                    )
                    stage1[b, p, delta].start()

    links = {}

    def link(axis, tile):
        lt[axis] = tile
        for delta in range(1, RING):
            n = axis * 3 + delta - 1
            links[axis, delta] = copy(lt.at[axis], lr.at[axis, delta - 1], sl.at[n], vl.at[n], peer(axis, delta))
            links[axis, delta].start()

    def unlink(axis):
        for delta in range(1, RING):
            links[axis, delta].wait_recv()
        tiles = [lt[axis]] + [lr[axis, i] for i in range(3)]
        top = functools.reduce(jnp.maximum, [t[0:1] for t in tiles])
        total = sum(jnp.exp(t[0:1] - top) * t[1:2] for t in tiles)
        return jnp.concatenate([top, total, jnp.zeros((6, LANES), F32)], axis=0)

    with scope("lm"):
        head.wait()
        both = lax.dot_general(q_ref[...], w_ref[...], (((1,), (1,)), ((), ())), preferred_element_type=F32)
        mine = jnp.where(core == 0, both[:ROWS], both[ROWS:])
        logits[...] = mine
        lm_top = jnp.max(mine, axis=1, keepdims=True)
        lm_sum = jnp.sum(jnp.exp(mine - lm_top), axis=1, keepdims=True)
        lane = lax.broadcasted_iota(jnp.int32, (ROWS, LANES), 1)
        pair = jnp.where(lane == 0, lm_top, lm_sum)
        pair = jnp.concatenate([pair] * GROUPS, axis=0).T
        link(0, pair[0:8, :])

    def combine(stats):
        m = functools.reduce(jnp.maximum, [s[0:1] for s in stats])
        scales = [jnp.exp(s[0:1] - m) for s in stats]
        zz = sum(c * s[1:2] for c, s in zip(scales, stats))
        return scales, jnp.concatenate([m, zz, jnp.zeros((STAT - 2, LANES), F32)], axis=0)

    def second(p, delta, to):
        n = p * 3 + delta - 1
        return copy(e.at[p, to], r2.at[p, delta - 1], s2.at[n], v2.at[n], peer(order[p][1], delta))

    factors = {}
    for b in range(RING):
        for p in range(PARTS):
            with scope("w1"):
                for delta in range(1, RING):
                    stage1[b, p, delta].wait_recv()
            own = p * RING + dims[order[p][0]][0]
            if b == 0:
                factors[p] = combine([d[own, 0:STAT, :]] + [r1[p, i, 0:STAT, :] for i in range(3)])
            scales, stats = factors[p]
            total = scales[0] * d[own, body(b), :]
            for i in range(3):
                total = total + scales[i + 1] * r1[p, i, body(b), :]
            e[p, b, 0:STAT, :] = stats
            e[p, b, STAT:MSG2, :] = total
            here = dims[order[p][1]][0]

            @pl.when(here != b)
            def _():
                second(p, (b - here + RING) % RING, b).start()

    link(1, unlink(0))

    def third(p, delta, to):
        n = p * 3 + delta - 1
        return copy(g3.at[p, to], r3.at[p, delta - 1], s3.at[n], v3.at[n], peer(order[p][2], delta))

    for p in range(PARTS):
        own = dims[order[p][1]][0]
        with scope("w2"):
            for delta in range(1, RING):
                second(p, delta, (own + delta) % RING).wait_recv()
        scales, stats = combine([e[p, own, 0:STAT, :]] + [r2[p, i, 0:STAT, :] for i in range(3)])
        for c in range(RING):
            rows = slice(STAT + c * SLOTS, STAT + (c + 1) * SLOTS)
            total = scales[0] * e[p, own, rows, :]
            for i in range(3):
                total = total + scales[i + 1] * r2[p, i, rows, :]
            g3[p, c, 0:SLOTS, :] = total
            g3[p, c, SLOTS:MSG3, :] = stats[0 : MSG3 - SLOTS]
        here = dims[order[p][2]][0]
        for delta in (2, 1, 3):
            third(p, delta, (here + delta) % RING).start()
    link(2, unlink(1))

    tsc[...] = jnp.zeros(tsc.shape, F32)
    slots = logits.shape[1] // GROUPS
    for p in range(PARTS):
        own = dims[order[p][2]][0]
        with scope("w3"):
            for delta in range(1, RING):
                third(p, delta, (own + delta) % RING).wait_recv()
        blocks = [g3[p, own]] + [r3[p, i] for i in range(3)]
        scales, stats = combine([v[SLOTS : SLOTS + 2] for v in blocks])
        count = min(SLOTS, slots - p * SLOTS)
        total = sum(c * v[0:count] for c, v in zip(scales, blocks))
        tsc[p * SLOTS : p * SLOTS + count, :] = total / stats[1:2]
    tsc[slots : slots + 2, :] = unlink(2)[0:2]

    with scope("final"):
        turned = tsc[...].T
        for g in range(GROUPS):
            knn[:, g * slots : (g + 1) * slots] = turned[g * ROWS : (g + 1) * ROWS, 0:slots]
        lm = jnp.exp(logits[...] - turned[0:ROWS, slots : slots + 1]) / turned[0:ROWS, slots + 1 : slots + 2]
        mix = mix_ref[0, 0]
        out_ref[...] = jnp.log(mix * knn[...] + (1.0 - mix) * lm)

    for sent in list(near.values()) + list(stage1.values()) + list(links.values()):
        sent.wait_send()
    for p in range(PARTS):
        for delta in range(1, RING):
            second(p, delta, (dims[order[p][1]][0] + delta) % RING).wait_send()
            third(p, delta, (dims[order[p][2]][0] + delta) % RING).wait_send()


def solution(mesh):
    def local_step(queries, w_head, store_keys, store_tok, temperature, mix_weight):
        n_keys, width = store_keys.shape
        vocab_loc = w_head.shape[1]
        vmem, smem, hbm = (pl.BlockSpec(memory_space=s) for s in (pltpu.VMEM, pltpu.SMEM, pltpu.HBM))

        in_hbm = lambda a: pltpu.with_memory_space_constraint(a, pltpu.HBM)
        *hist, stats = pl.pallas_call(
            functools.partial(local_kernel, vocab_loc),
            out_shape=[jax.ShapeDtypeStruct((HROWS, LANES), F32)] * NBUF + [jax.ShapeDtypeStruct((2 * NBUF, 2 * LANES), F32)],
            in_specs=[smem, hbm, hbm, hbm],
            out_specs=[vmem] * (NBUF + 1),
            scratch_shapes=[
                pltpu.VMEM(queries.shape, jnp.bfloat16),
                pltpu.VMEM(store_keys.shape, jnp.bfloat16),
                pltpu.VMEM((2 * LANES, width), jnp.bfloat16),
                pltpu.VMEM((n_keys // NBUF, 2 * LANES), F32),
                pltpu.VMEM((2 * n_keys, LANES), F32),
                pltpu.VMEM((n_keys, LANES), F32),
                pltpu.VMEM((n_keys // LANES, LANES), jnp.int32),
                pltpu.SMEM((n_keys // LANES, LANES), jnp.int32),
                pltpu.VMEM((n_keys // LANES, LANES), jnp.int32),
                pltpu.SemaphoreType.DMA,
                pltpu.SemaphoreType.DMA,
                pltpu.SemaphoreType.DMA,
                pltpu.SemaphoreType.DMA((2 * NBUF,)),
            ],
            compiler_params=pltpu.CompilerParams(vmem_limit_bytes=KA_LIMIT * 2**20),
            name="histogram",
        )(temperature.reshape(1, 1), in_hbm(store_tok.reshape(n_keys // LANES, LANES)), in_hbm(queries), in_hbm(store_keys))

        return pl.pallas_call(
            comm_kernel,
            out_shape=jax.ShapeDtypeStruct((ROWS, vocab_loc), F32),
            in_specs=[smem] + [vmem] * (NBUF + 2) + [hbm],
            out_specs=vmem,
            scratch_shapes=[
                pltpu.VMEM(w_head.shape[::-1], jnp.bfloat16),
                pltpu.VMEM((ROWS, vocab_loc), F32),
                pltpu.VMEM((2, PARTS * RING, MSG, LANES), F32),
                pltpu.VMEM((PARTS * RING, MSG, LANES), F32),
                pltpu.VMEM((PARTS * RING, MSG, LANES), F32),
                pltpu.VMEM((PARTS, RING - 1, MSG, LANES), F32),
                pltpu.VMEM((PARTS, RING, MSG2, LANES), F32),
                pltpu.VMEM((PARTS, RING - 1, MSG2, LANES), F32),
                pltpu.VMEM((PARTS, RING, MSG3, LANES), F32),
                pltpu.VMEM((PARTS, RING - 1, MSG3, LANES), F32),
                pltpu.VMEM((3, STAT, LANES), F32),
                pltpu.VMEM((3, RING - 1, STAT, LANES), F32),
                pltpu.VMEM((LANES, LANES), F32),
                pltpu.VMEM((ROWS, vocab_loc), F32),
                pltpu.SemaphoreType.DMA,
                pltpu.SemaphoreType.DMA((12,)),
                pltpu.SemaphoreType.DMA((12,)),
                pltpu.SemaphoreType.DMA((36,)),
                pltpu.SemaphoreType.DMA((36,)),
            ]
            + [pltpu.SemaphoreType.DMA((9,))] * 6,
            compiler_params=pltpu.CompilerParams(collective_id=0, has_side_effects=True, vmem_limit_bytes=KB_LIMIT * 2**20),
            name="exchange",
        )(mix_weight.reshape(1, 1), *hist, stats, queries, in_hbm(w_head.T))

    return jax.shard_map(
        local_step,
        mesh=mesh,
        in_specs=(P("data", None), P(None, "model"), P(("store", "model"), None), P(("store", "model")), P(), P()),
        out_specs=P(("data", "store"), "model"),
        check_vma=False,
    )
```

time: 549 us -> 45.2 us (0.08)
  the two profiles are of different devices: /device:TPU:1 before, /device:TPU:6 now
where the time goes in v3:
time: 45.2 us; the launch traced here: 45.1 us
  Pallas kernels  43.2 us (96%)
  between operations  1.33 us (3%)
  local copies, waits for them, and re-layouts  0.62 us (1%)
    pallas_call x1, Pallas kernels, local_step(): pl.pallas_call(comm_kernel, out_shape=jax.ShapeDtypeStruct((ROWS, vocab_l...  26.9 us
    pallas_call x1, Pallas kernels, local_step(): pl.pallas_call(functools.partial(local_kernel, vocab_loc), out_shape=[jax...  16.2 us

profile of v3, /device:TPU:6, one launch (start us, length us, event | category | flops | bytes accessed | tf_op | source)
XLA Modules:
  0.0 45.1 jit_solution(4192282386405335263)
XLA Ops:
  1.3 0.0 copy-start
  1.3 16.2 %histogram.1 = (f32[6912,128]{1,0:T(8,128)S(1)}, f32[6912,128]{1,0:T(8,128)S(1)}, f32[6912,128]{1,0:T(8,128)S(1)}, f32[6912,128]{1,0:T(8,128)S(1)}, f32[8,256]{1,0:T(8,128)S(1)}) custom-call(f32[1,1]{1,0:T(1,128)} %bitcast.4.tau_ref, s32[16,128]{1,0:T(8,128)} %bitcast.7, bf16[16,2560]{1,0:T(8,128)(2,1)} %q_ref.1, bf16[2048,2560]{1,0:T(8,128)(2,1)} %k_hbm.1), custom_call_target="tpu_custom_call" | custom-call | tf_op jit(solution)/shard_map/histogram/pallas_call | solution.py:338
  17.5 0.0 copy-done
  17.5 26.9 %exchange.1 = f32[8,800]{1,0:T(8,128)S(1)} custom-call(f32[1,1]{1,0:T(1,128)} %bitcast.5.mix_ref, f32[6912,128]{1,0:T(8,128)S(1)} %get-tuple-element.10.h0, f32[6912,128]{1,0:T(8,128)S(1)} %get-tuple-element.11.h1, f32[6912,128]{1,0:T(8,128)S(1)} %get-tuple-element.12.h2, f32[6912,128]{1,0:T(8,128)S(1)} %get-tuple-element.13.h3, ...), custom_call_target="tpu_custom_call" | custom-call | tf_op jit(solution)/shard_map/exchange/pallas_call | solution.py:362
  44.5 0.6 %copy.10 = f32[8,800]{1,0:T(8,128)} copy(f32[8,800]{1,0:T(8,128)S(1)} %exchange.1) | data formatting | bytes 51200
Async XLA Ops:
  1.3 16.2 %copy-start = (bf16[16,2560]{1,0:T(8,128)(2,1)S(1)}, bf16[16,2560]{1,0:T(8,128)(2,1)}, u32[]{:S(2)}) copy-start(bf16[16,2560]{1,0:T(8,128)(2,1)} %q_ref.1) | copy-start | bytes 245764

commit v4 on v3

v4 whole, which is shorter than its diff:
```python
import functools

import jax
import jax.numpy as jnp
from jax import lax
from jax.experimental import pallas as pl
from jax.experimental.pallas import tpu as pltpu
from jax.sharding import PartitionSpec as P

F32 = jnp.float32
LANES = 128
RING = 4
CHIPS = RING**3
ROWS = 8
GROUPS = LANES // ROWS
SLOTS = 18
PARTS = 3
BLOCK = SLOTS * CHIPS // RING
BLOCK2 = BLOCK // RING
STAT = 8
MSG = STAT + BLOCK
MSG2 = STAT + BLOCK2
MSG3 = 24
NBUF = 4
KA_LIMIT = 36
KB_LIMIT = 36
HROWS = 2 * SLOTS * CHIPS * PARTS
MESH = pl.DeviceIdType.MESH
scope = jax.named_scope


def below(a, n):
    return ((a.astype(F32) + 0.5) * (1.0 / n)).astype(jnp.int32)


def local_kernel(vocab_loc, tau_ref, tok_hbm, q_hbm, k_hbm, *refs):
    hist, stats_ref = refs[:NBUF], refs[NBUF]
    q_ref, k_ref, qrep, sc, wx, grp, idx, idx_smem, tok_ref, qsem, isem, tsem, ksem = refs[NBUF + 1 :]
    n_keys = k_ref.shape[0]
    quarter = n_keys // NBUF
    chunk = quarter // 2

    def fetch(j):
        rows = pl.ds(pl.multiple_of(j * chunk, chunk), chunk)
        return pltpu.make_async_copy(k_hbm.at[rows], k_ref.at[rows], ksem.at[j])

    get_tok = pltpu.make_async_copy(tok_hbm, tok_ref, tsem)
    get_tok.start()
    get_q = pltpu.make_async_copy(q_hbm, q_ref, qsem)
    get_q.start()
    for j in range(2):
        fetch(j).start()
    span = 288
    pieces = HROWS // span // 3

    for third in range(3):

        @pl.loop(third * pieces, (third + 1) * pieces)
        def _(i):
            for buf in hist:
                buf[pl.ds(pl.multiple_of(i * span, 8), span), :] = jnp.zeros((span, LANES), F32)

        for j in range(2 + third * 2, 4 + third * 2):
            fetch(j).start()

    get_tok.wait()
    with scope("index"):
        tok = tok_ref[...]
        chip = below(tok, vocab_loc)
        within = tok - chip * vocab_loc
        slots = vocab_loc // GROUPS
        group = below(within, slots)
        slot = within - group * slots
        part = (slot >= SLOTS).astype(jnp.int32) + (slot >= 2 * SLOTS).astype(jnp.int32)
        row = slot - part * SLOTS
        x, y, z = chip & 3, (chip >> 2) & 3, chip >> 4
        first = jnp.where(part == 0, x, jnp.where(part == 1, y, z))
        second = jnp.where(part == 0, y, jnp.where(part == 1, z, x))
        third = jnp.where(part == 0, z, jnp.where(part == 1, x, y))
        place = ((part * RING + first) * RING + second) * RING + third
        idx[...] = (place * SLOTS + row) * 2
        put_idx = pltpu.make_async_copy(idx, idx_smem, isem)
        put_idx.start()
    with scope("mask"):
        group = group.astype(F32)
        square = (LANES, LANES)
        eye = lax.broadcasted_iota(jnp.int32, square, 0) == lax.broadcasted_iota(jnp.int32, square, 1)
        ones = jnp.ones(square, jnp.bfloat16)
        for c in range(n_keys // LANES):
            spread = jnp.where(eye, jnp.broadcast_to(group[c : c + 1, :], square), 0.0).astype(jnp.bfloat16)
            grp[c * LANES : (c + 1) * LANES, :] = jnp.dot(spread, ones, preferred_element_type=F32)

    with scope("turn"):
        get_q.wait()
        pick = (2 * ROWS, 2 * LANES)
        lane = lax.broadcasted_iota(jnp.int32, pick, 1)
        pick = lax.broadcasted_iota(jnp.int32, pick, 0) == (lane // LANES) * ROWS + lane % ROWS
        pick = pick.astype(F32).astype(jnp.bfloat16)
        wide = 512
        for c in range(0, q_ref.shape[1], wide):
            turned = lax.dot_general(q_ref[:, c : c + wide], pick, (((0,), (0,)), ((), ())), preferred_element_type=F32)
            qrep[c : c + wide, :] = turned.astype(jnp.bfloat16)

    inv = 1.0 / tau_ref[0, 0]
    lane_group = (lax.broadcasted_iota(jnp.int32, (LANES, LANES), 1) // ROWS).astype(F32)

    @pl.loop(0, NBUF)
    def _(b):
        with scope("kw"):
            for sub in range(2):
                fetch(b * 2 + sub).wait()
        with scope("dots"):
            keys = k_ref[pl.ds(pl.multiple_of(b * quarter, quarter), quarter), :]
            dots = jnp.dot(keys, qrep[...], preferred_element_type=F32)
            kf = keys.astype(F32)
            norms = jnp.sum(kf * kf, axis=1, keepdims=True)
            scores = (2.0 * dots - norms) * inv
            sc[...] = scores
            top = jnp.max(scores.reshape(quarter // 8, 8, 2 * LANES), axis=0)
            m = jnp.max(top, axis=0, keepdims=True)
        with scope("expand"):
            total = jnp.zeros((8, 2 * LANES), F32)
            for c in range(quarter // LANES):
                w = jnp.exp(sc[c * LANES : (c + 1) * LANES, :] - m)
                total = total + jnp.sum(w.reshape(LANES // 8, 8, 2 * LANES), axis=0)
                at = b * quarter + c * LANES
                mine = grp[pl.ds(pl.multiple_of(at, LANES), LANES), :] == lane_group
                for h in range(2):
                    wx[pl.ds(at * 2 + h, LANES, stride=2), :] = jnp.where(mine, w[:, h * LANES : (h + 1) * LANES], 0.0)
            total = jnp.sum(total, axis=0, keepdims=True)
            stats_ref[pl.ds(b, 1), :] = m
            stats_ref[pl.ds(NBUF + b, 1), :] = total

    put_idx.wait()
    unroll = 8
    rows = quarter // LANES
    with scope("scatter"):
        for c in range(rows):

            @pl.loop(0, LANES // unroll)
            def _(i):
                for u in range(unroll):
                    lane = i * unroll + u
                    at = [pl.ds(pl.multiple_of(idx_smem[b * rows + c, lane], 2), 2) for b in range(NBUF)]
                    new = [
                        hist[b][at[b], :] + wx[pl.ds(pl.multiple_of(((b * rows + c) * LANES + lane) * 2, 2), 2), :]
                        for b in range(NBUF)
                    ]
                    for b in range(NBUF):
                        hist[b][at[b], :] = new[b]


def comm_kernel(
    mix_ref, h0, h1, h2, h3, kstats, q_ref, w_hbm, out_ref,
    w_ref, logits, loc, din, d, r1, e, r2, g3, r3, lt, lr, tsc, knn,
    wsem, s0, v0, s1, v1, s2, v2, s3, v3, sl, vl,
):
    core = lax.axis_index("store")
    chip = lax.axis_index("model")
    x, y, z = chip % RING, (chip // RING) % RING, chip // (RING * RING)
    dims = ((x, 1), (y, RING), (z, RING * RING))
    order = ((0, 1, 2), (1, 2, 0), (2, 0, 1))

    def peer(axis, delta):
        at, stride = dims[axis]
        return {"model": chip + ((at + delta) % RING - at) * stride}

    barrier = pltpu.get_barrier_semaphore()
    pl.semaphore_signal(barrier, inc=1, device_id={"store": 1 - core}, device_id_type=MESH)
    for axis in range(3):
        for delta in range(1, RING):
            pl.semaphore_signal(barrier, inc=1, device_id=peer(axis, delta), device_id_type=MESH)
    head = pltpu.make_async_copy(w_hbm, w_ref, wsem)
    head.start()

    hist = (h0, h1, h2, h3)
    top = functools.reduce(jnp.maximum, [kstats[b : b + 1, :] for b in range(NBUF)])
    scales = [jnp.exp(kstats[b : b + 1, :] - top) for b in range(NBUF)]
    mass = sum(c * kstats[NBUF + b : NBUF + b + 1, :] for b, c in enumerate(scales))
    half = [slice(h * LANES, (h + 1) * LANES) for h in range(2)]

    with scope("sum"):

        @pl.loop(0, PARTS * RING)
        def _(blk):
            for h in range(2):
                loc[h, blk, 0:STAT, :] = jnp.concatenate(
                    [top[:, half[h]], mass[:, half[h]], jnp.zeros((STAT - 2, LANES), F32)], axis=0
                )
                for t in range(BLOCK // 8):
                    at = pl.ds(blk * 2 * BLOCK + t * 16 + h, 8, stride=2)
                    total = scales[0][:, half[h]] * hist[0][at, :]
                    for b in range(1, NBUF):
                        total = total + scales[b][:, half[h]] * hist[b][at, :]
                    loc[h, blk, STAT + t * 8 : STAT + t * 8 + 8, :] = total

    with scope("barrier"):
        pl.semaphore_wait(barrier, 10)

    def copy(src, dst, ssem, rsem, to):
        return pltpu.make_async_remote_copy(src_ref=src, dst_ref=dst, send_sem=ssem, recv_sem=rsem, device_id=to, device_id_type=MESH)

    def span(b):
        return slice(0, MSG2) if b == 0 else slice(STAT + b * BLOCK2, STAT + (b + 1) * BLOCK2)

    def body(b):
        return slice(STAT + b * BLOCK2, STAT + (b + 1) * BLOCK2)

    partner = {"store": 1 - core}
    first = [dims[order[p][0]][0] for p in range(PARTS)]
    mid = [dims[order[p][1]][0] for p in range(PARTS)]
    last = [dims[order[p][2]][0] for p in range(PARTS)]

    def near(b, p):
        blks = slice(p * RING, (p + 1) * RING)
        return copy(loc.at[1 - core, blks, span(b)], din.at[blks, span(b)], s0, v0.at[b * PARTS + p], partner)

    for b in range(RING):
        for p in range(PARTS):
            near(b, p).start()

    def link(axis, tile):
        lt[axis] = tile
        for delta in range(1, RING):
            copy(lt.at[axis], lr.at[axis, delta - 1], sl, vl.at[axis], peer(axis, delta)).start()

    def unlink(axis):
        copy(lr.at[axis], lr.at[axis], sl, vl.at[axis], partner).wait_recv()
        tiles = [lt[axis]] + [lr[axis, i] for i in range(3)]
        top = functools.reduce(jnp.maximum, [t[0:1] for t in tiles])
        total = sum(jnp.exp(t[0:1] - top) * t[1:2] for t in tiles)
        return jnp.concatenate([top, total, jnp.zeros((6, LANES), F32)], axis=0)

    for b in range(RING):
        for p in range(PARTS):
            with scope("w0"):
                near(b, p).wait_recv()
            if b == 0 and p == 0:
                m_own, m_par = loc[core, 0, 0:1, :], din[0, 0:1, :]
                m = jnp.maximum(m_own, m_par)
                c_own, c_par = jnp.exp(m_own - m), jnp.exp(m_par - m)
                zz = c_own * loc[core, 0, 1:2, :] + c_par * din[0, 1:2, :]
                stats = jnp.concatenate([m, zz, jnp.zeros((STAT - 2, LANES), F32)], axis=0)
            for delta in (2, 1, 3, 0):
                blk = p * RING + (first[p] + delta) % RING
                if b == 0:
                    d[blk, 0:STAT, :] = stats
                d[blk, body(b), :] = c_own * loc[core, blk, body(b), :] + c_par * din[blk, body(b), :]
                if delta:
                    to = peer(order[p][0], delta)
                    copy(d.at[blk, span(b)], r1.at[p, delta - 1, span(b)], s1, v1.at[b * PARTS + p], to).start()

        if b == 0:
            with scope("lm"):
                head.wait()
                both = lax.dot_general(q_ref[...], w_ref[...], (((1,), (1,)), ((), ())), preferred_element_type=F32)
                mine = jnp.where(core == 0, both[:ROWS], both[ROWS:])
                logits[...] = mine
                lm_top = jnp.max(mine, axis=1, keepdims=True)
                lm_sum = jnp.sum(jnp.exp(mine - lm_top), axis=1, keepdims=True)
                lane = lax.broadcasted_iota(jnp.int32, (ROWS, LANES), 1)
                pair = jnp.where(lane == 0, lm_top, lm_sum)
                pair = jnp.concatenate([pair] * GROUPS, axis=0).T
                link(0, pair[0:8, :])

    def combine(stats):
        m = functools.reduce(jnp.maximum, [s[0:1] for s in stats])
        scales = [jnp.exp(s[0:1] - m) for s in stats]
        zz = sum(c * s[1:2] for c, s in zip(scales, stats))
        return scales, jnp.concatenate([m, zz, jnp.zeros((STAT - 2, LANES), F32)], axis=0)

    factors = {}
    for b in range(RING):
        for p in range(PARTS):
            with scope("w1"):
                dst = r1.at[p, :, span(b)]
                copy(dst, dst, s1, v1.at[b * PARTS + p], partner).wait_recv()
            own = p * RING + first[p]
            if b == 0:
                factors[p] = combine([d[own, 0:STAT, :]] + [r1[p, i, 0:STAT, :] for i in range(3)])
            scales, stats = factors[p]
            total = scales[0] * d[own, body(b), :]
            for i in range(3):
                total = total + scales[i + 1] * r1[p, i, body(b), :]
            e[p, b, 0:STAT, :] = stats
            e[p, b, STAT:MSG2, :] = total

            @pl.when(mid[p] != b)
            def _():
                delta = (b - mid[p] + RING) % RING
                copy(e.at[p, b], r2.at[p, delta - 1], s2, v2.at[p], peer(order[p][1], delta)).start()

        if b == 1:
            link(1, unlink(0))
        if b == 3:
            link(2, unlink(1))

    for p in range(PARTS):
        with scope("w2"):
            copy(r2.at[p], r2.at[p], s2, v2.at[p], partner).wait_recv()
        own = mid[p]
        scales, stats = combine([e[p, own, 0:STAT, :]] + [r2[p, i, 0:STAT, :] for i in range(3)])
        for c in range(RING):
            rows = slice(STAT + c * SLOTS, STAT + (c + 1) * SLOTS)
            total = scales[0] * e[p, own, rows, :]
            for i in range(3):
                total = total + scales[i + 1] * r2[p, i, rows, :]
            g3[p, c, 0:SLOTS, :] = total
            g3[p, c, SLOTS:MSG3, :] = stats[0 : MSG3 - SLOTS]
        for delta in (2, 1, 3):
            to = (last[p] + delta) % RING
            copy(g3.at[p, to], r3.at[p, delta - 1], s3, v3.at[p], peer(order[p][2], delta)).start()

    slots = logits.shape[1] // GROUPS
    mix = mix_ref[0, 0]
    with scope("lm2"):
        tsc[...] = jnp.zeros(tsc.shape, F32)
        tsc[0:STAT, :] = unlink(2)
        turned = tsc[...].T
        lm = jnp.exp(logits[...] - turned[0:ROWS, 0:1]) / turned[0:ROWS, 1:2]
        logits[...] = (1.0 - mix) * lm
        copy(loc.at[1 - core], din, s0, v0.at[0], partner).wait_send()
        copy(r1, r1, s1, v1.at[0], partner).wait_send()
        copy(r2, r2, s2, v2.at[0], partner).wait_send()
        copy(lr, lr, sl, vl.at[0], partner).wait_send()

    for p in range(PARTS):
        with scope("w3"):
            copy(r3.at[p], r3.at[p], s3, v3.at[p], partner).wait_recv()
        blocks = [g3[p, last[p]]] + [r3[p, i] for i in range(3)]
        scales, stats = combine([v[SLOTS : SLOTS + 2] for v in blocks])
        count = min(SLOTS, slots - p * SLOTS)
        total = sum(c * v[0:count] for c, v in zip(scales, blocks))
        tsc[p * SLOTS : p * SLOTS + count, :] = total / stats[1:2]

    with scope("final"):
        turned = tsc[...].T
        for g in range(GROUPS):
            knn[:, g * slots : (g + 1) * slots] = turned[g * ROWS : (g + 1) * ROWS, 0:slots]
        out_ref[...] = jnp.log(mix * knn[...] + logits[...])

    copy(r3, r3, s3, v3.at[0], partner).wait_send()


def solution(mesh):
    def local_step(queries, w_head, store_keys, store_tok, temperature, mix_weight):
        n_keys, width = store_keys.shape
        vocab_loc = w_head.shape[1]
        vmem, smem, hbm = (pl.BlockSpec(memory_space=s) for s in (pltpu.VMEM, pltpu.SMEM, pltpu.HBM))

        in_hbm = lambda a: pltpu.with_memory_space_constraint(a, pltpu.HBM)
        *hist, stats = pl.pallas_call(
            functools.partial(local_kernel, vocab_loc),
            out_shape=[jax.ShapeDtypeStruct((HROWS, LANES), F32)] * NBUF + [jax.ShapeDtypeStruct((2 * NBUF, 2 * LANES), F32)],
            in_specs=[smem, hbm, hbm, hbm],
            out_specs=[vmem] * (NBUF + 1),
            scratch_shapes=[
                pltpu.VMEM(queries.shape, jnp.bfloat16),
                pltpu.VMEM(store_keys.shape, jnp.bfloat16),
                pltpu.VMEM((width, 2 * LANES), jnp.bfloat16),
                pltpu.VMEM((n_keys // NBUF, 2 * LANES), F32),
                pltpu.VMEM((2 * n_keys, LANES), F32),
                pltpu.VMEM((n_keys, LANES), F32),
                pltpu.VMEM((n_keys // LANES, LANES), jnp.int32),
                pltpu.SMEM((n_keys // LANES, LANES), jnp.int32),
                pltpu.VMEM((n_keys // LANES, LANES), jnp.int32),
                pltpu.SemaphoreType.DMA,
                pltpu.SemaphoreType.DMA,
                pltpu.SemaphoreType.DMA,
                pltpu.SemaphoreType.DMA((2 * NBUF,)),
            ],
            compiler_params=pltpu.CompilerParams(vmem_limit_bytes=KA_LIMIT * 2**20),
            name="histogram",
        )(temperature.reshape(1, 1), in_hbm(store_tok.reshape(n_keys // LANES, LANES)), in_hbm(queries), in_hbm(store_keys))

        return pl.pallas_call(
            comm_kernel,
            out_shape=jax.ShapeDtypeStruct((ROWS, vocab_loc), F32),
            in_specs=[smem] + [vmem] * (NBUF + 2) + [hbm],
            out_specs=vmem,
            scratch_shapes=[
                pltpu.VMEM(w_head.shape[::-1], jnp.bfloat16),
                pltpu.VMEM((ROWS, vocab_loc), F32),
                pltpu.VMEM((2, PARTS * RING, MSG, LANES), F32),
                pltpu.VMEM((PARTS * RING, MSG, LANES), F32),
                pltpu.VMEM((PARTS * RING, MSG, LANES), F32),
                pltpu.VMEM((PARTS, RING - 1, MSG, LANES), F32),
                pltpu.VMEM((PARTS, RING, MSG2, LANES), F32),
                pltpu.VMEM((PARTS, RING - 1, MSG2, LANES), F32),
                pltpu.VMEM((PARTS, RING, MSG3, LANES), F32),
                pltpu.VMEM((PARTS, RING - 1, MSG3, LANES), F32),
                pltpu.VMEM((3, STAT, LANES), F32),
                pltpu.VMEM((3, RING - 1, STAT, LANES), F32),
                pltpu.VMEM((LANES, LANES), F32),
                pltpu.VMEM((ROWS, vocab_loc), F32),
                pltpu.SemaphoreType.DMA,
                pltpu.SemaphoreType.DMA,
                pltpu.SemaphoreType.DMA((12,)),
                pltpu.SemaphoreType.DMA,
                pltpu.SemaphoreType.DMA((12,)),
            ]
            + [pltpu.SemaphoreType.DMA, pltpu.SemaphoreType.DMA((3,))] * 3,
            compiler_params=pltpu.CompilerParams(collective_id=0, has_side_effects=True, vmem_limit_bytes=KB_LIMIT * 2**20),
            name="exchange",
        )(mix_weight.reshape(1, 1), *hist, stats, queries, in_hbm(w_head.T))

    return jax.shard_map(
        local_step,
        mesh=mesh,
        in_specs=(P("data", None), P(None, "model"), P(("store", "model"), None), P(("store", "model")), P(), P()),
        out_specs=P(("data", "store"), "model"),
        check_vma=False,
    )
```

time: 45.2 us -> 36.9 us (0.82)
  Pallas kernels: 43.2 us -> 34.9 us
    pallas_call x1, Pallas kernels: 16.2 us -> 9.23 us  [local_step(): pl.pallas_call(functools.partial(local_kernel, vocab_loc), out_shape=[jax...]
    pallas_call x1, Pallas kernels: 26.9 us -> 25.6 us  [local_step(): pl.pallas_call(comm_kernel, out_shape=jax.ShapeDtypeStruct((ROWS, vocab_l...]
where the time goes in v4:
time: 36.9 us; the launch traced here: 36.8 us
  Pallas kernels  34.9 us (95%)
  between operations  1.33 us (4%)
  local copies, waits for them, and re-layouts  0.62 us (2%)
    pallas_call x1, Pallas kernels, local_step(): pl.pallas_call(comm_kernel, out_shape=jax.ShapeDtypeStruct((ROWS, vocab_l...  25.6 us
    pallas_call x1, Pallas kernels, local_step(): pl.pallas_call(functools.partial(local_kernel, vocab_loc), out_shape=[jax...  9.23 us

profile of v4, /device:TPU:6, one launch (start us, length us, event | category | flops | bytes accessed | tf_op | source)
XLA Modules:
  0.0 36.8 jit_solution(750744121542567721)
XLA Ops:
  1.3 0.0 copy-start
  1.3 9.2 %histogram.1 = (f32[6912,128]{1,0:T(8,128)S(1)}, f32[6912,128]{1,0:T(8,128)S(1)}, f32[6912,128]{1,0:T(8,128)S(1)}, f32[6912,128]{1,0:T(8,128)S(1)}, f32[8,256]{1,0:T(8,128)S(1)}) custom-call(f32[1,1]{1,0:T(1,128)} %bitcast.4.tau_ref, s32[16,128]{1,0:T(8,128)} %bitcast.7, bf16[16,2560]{1,0:T(8,128)(2,1)} %q_ref.1, bf16[2048,2560]{1,0:T(8,128)(2,1)} %k_hbm.1), custom_call_target="tpu_custom_call" | custom-call | tf_op jit(solution)/shard_map/histogram/pallas_call | solution.py:352
  10.5 0.0 copy-done
  10.6 25.6 %exchange.1 = f32[8,800]{1,0:T(8,128)S(1)} custom-call(f32[1,1]{1,0:T(1,128)} %bitcast.5.mix_ref, f32[6912,128]{1,0:T(8,128)S(1)} %get-tuple-element.10.h0, f32[6912,128]{1,0:T(8,128)S(1)} %get-tuple-element.11.h1, f32[6912,128]{1,0:T(8,128)S(1)} %get-tuple-element.12.h2, f32[6912,128]{1,0:T(8,128)S(1)} %get-tuple-element.13.h3, ...), custom_call_target="tpu_custom_call" | custom-call | tf_op jit(solution)/shard_map/exchange/pallas_call | solution.py:376
  36.2 0.6 %copy.10 = f32[8,800]{1,0:T(8,128)} copy(f32[8,800]{1,0:T(8,128)S(1)} %exchange.1) | data formatting | bytes 51200
Async XLA Ops:
  1.3 9.2 %copy-start = (bf16[16,2560]{1,0:T(8,128)(2,1)S(1)}, bf16[16,2560]{1,0:T(8,128)(2,1)}, u32[]{:S(2)}) copy-start(bf16[16,2560]{1,0:T(8,128)(2,1)} %q_ref.1) | copy-start | bytes 245764

commit v5 on v4

--- a/solution.py
+++ b/solution.py
@@ -21,6 +21,8 @@
 MSG = STAT + BLOCK
 MSG2 = STAT + BLOCK2
 MSG3 = 24
+LEAD = 40
+HEAVY = 40
 NBUF = 4
 KA_LIMIT = 36
 KB_LIMIT = 36
@@ -152,8 +154,8 @@
 
 def comm_kernel(
     mix_ref, h0, h1, h2, h3, kstats, q_ref, w_hbm, out_ref,
-    w_ref, logits, loc, din, d, r1, e, r2, g3, r3, lt, lr, tsc, knn,
-    wsem, s0, v0, s1, v1, s2, v2, s3, v3, sl, vl,
+    w_ref, logits, loc, din, d, ra, rb, rc, rd, e, r2, g3, r3, lt, lr, tsc, knn,
+    wsem, s0, v0, s1, va, vb, vc, s2, v2, s3, v3, sl, vl,
 ):
     core = lax.axis_index("store")
     chip = lax.axis_index("model")
@@ -184,7 +186,7 @@
         @pl.loop(0, PARTS * RING)
         def _(blk):
             for h in range(2):
-                loc[h, blk, 0:STAT, :] = jnp.concatenate(
+                loc[h, blk, LEAD : LEAD + STAT, :] = jnp.concatenate(
                     [top[:, half[h]], mass[:, half[h]], jnp.zeros((STAT - 2, LANES), F32)], axis=0
                 )
                 for t in range(BLOCK // 8):
@@ -192,7 +194,8 @@
                     total = scales[0][:, half[h]] * hist[0][at, :]
                     for b in range(1, NBUF):
                         total = total + scales[b][:, half[h]] * hist[b][at, :]
-                    loc[h, blk, STAT + t * 8 : STAT + t * 8 + 8, :] = total
+                    row = t * 8 if t * 8 < LEAD else t * 8 + STAT
+                    loc[h, blk, row : row + 8, :] = total
 
     with scope("barrier"):
         pl.semaphore_wait(barrier, 10)
@@ -203,21 +206,42 @@
     def span(b):
         return slice(0, MSG2) if b == 0 else slice(STAT + b * BLOCK2, STAT + (b + 1) * BLOCK2)
 
-    def body(b):
-        return slice(STAT + b * BLOCK2, STAT + (b + 1) * BLOCK2)
-
+    def piece(b, half):
+        cut = HEAVY if b % 2 == 0 else BLOCK2 - HEAVY
+        start = STAT + b * BLOCK2
+        if b == 0:
+            return slice(0, LEAD) if half == 0 else slice(LEAD + STAT, MSG2)
+        return slice(start, start + cut) if half == 0 else slice(start + cut, start + BLOCK2)
+
+    def parcel(b, half):
+        if b == 0:
+            return slice(0, LEAD + STAT) if half == 0 else slice(LEAD, MSG2)
+        return piece(b, half)
+
+    tile = slice(LEAD, LEAD + STAT)
+    toward = (1, RING - 1)
     partner = {"store": 1 - core}
     first = [dims[order[p][0]][0] for p in range(PARTS)]
     mid = [dims[order[p][1]][0] for p in range(PARTS)]
     last = [dims[order[p][2]][0] for p in range(PARTS)]
 
-    def near(b, p):
-        blks = slice(p * RING, (p + 1) * RING)
-        return copy(loc.at[1 - core, blks, span(b)], din.at[blks, span(b)], s0, v0.at[b * PARTS + p], partner)
-
-    for b in range(RING):
+    def place(p, delta):
+        return p * RING + (first[p] + delta) % RING
+
+    def near(p, delta):
+        blk = place(p, delta)
+        return copy(loc.at[1 - core, blk], din.at[blk], s0, v0.at[p * RING + delta], partner)
+
+    for delta in (2, 1, 3, 0):
         for p in range(PARTS):
-            near(b, p).start()
+            near(p, delta).start()
+
+    def slot_of(b, p, half):
+        return (b * PARTS + p) * 2 + half
+
+    def incoming(dst, sem, b, p, half):
+        ref = dst.at[half, p, parcel(b, half)]
+        copy(ref, ref, s1, sem.at[slot_of(b, p, half)], partner).wait_recv()
 
     def link(axis, tile):
         lt[axis] = tile
@@ -231,69 +255,97 @@
         total = sum(jnp.exp(t[0:1] - top) * t[1:2] for t in tiles)
         return jnp.concatenate([top, total, jnp.zeros((6, LANES), F32)], axis=0)
 
-    for b in range(RING):
-        for p in range(PARTS):
-            with scope("w0"):
-                near(b, p).wait_recv()
-            if b == 0 and p == 0:
-                m_own, m_par = loc[core, 0, 0:1, :], din[0, 0:1, :]
-                m = jnp.maximum(m_own, m_par)
-                c_own, c_par = jnp.exp(m_own - m), jnp.exp(m_par - m)
-                zz = c_own * loc[core, 0, 1:2, :] + c_par * din[0, 1:2, :]
-                stats = jnp.concatenate([m, zz, jnp.zeros((STAT - 2, LANES), F32)], axis=0)
-            for delta in (2, 1, 3, 0):
-                blk = p * RING + (first[p] + delta) % RING
-                if b == 0:
-                    d[blk, 0:STAT, :] = stats
-                d[blk, body(b), :] = c_own * loc[core, blk, body(b), :] + c_par * din[blk, body(b), :]
-                if delta:
-                    to = peer(order[p][0], delta)
-                    copy(d.at[blk, span(b)], r1.at[p, delta - 1, span(b)], s1, v1.at[b * PARTS + p], to).start()
-
-        if b == 0:
-            with scope("lm"):
-                head.wait()
-                both = lax.dot_general(q_ref[...], w_ref[...], (((1,), (1,)), ((), ())), preferred_element_type=F32)
-                mine = jnp.where(core == 0, both[:ROWS], both[ROWS:])
-                logits[...] = mine
-                lm_top = jnp.max(mine, axis=1, keepdims=True)
-                lm_sum = jnp.sum(jnp.exp(mine - lm_top), axis=1, keepdims=True)
-                lane = lax.broadcasted_iota(jnp.int32, (ROWS, LANES), 1)
-                pair = jnp.where(lane == 0, lm_top, lm_sum)
-                pair = jnp.concatenate([pair] * GROUPS, axis=0).T
-                link(0, pair[0:8, :])
-
     def combine(stats):
         m = functools.reduce(jnp.maximum, [s[0:1] for s in stats])
         scales = [jnp.exp(s[0:1] - m) for s in stats]
         zz = sum(c * s[1:2] for c, s in zip(scales, stats))
         return scales, jnp.concatenate([m, zz, jnp.zeros((STAT - 2, LANES), F32)], axis=0)
 
+    chipwise = []
+
+    def issue(delta):
+        for p in range(PARTS):
+            blk = place(p, delta)
+            with scope("w0"):
+                near(p, delta).wait_recv()
+            if not chipwise:
+                chipwise.append(combine([loc[core, 0, tile, :], din[blk, tile, :]]))
+            (c_own, c_par), stats = chipwise[0]
+            d[blk, tile, :] = stats
+            for b in range(RING):
+                for half in range(2):
+                    rows = piece(b, half)
+                    d[blk, rows, :] = c_own * loc[core, blk, rows, :] + c_par * din[blk, rows, :]
+                    n, send = slot_of(b, p, half), parcel(b, half)
+                    if delta == 2:
+                        to = peer(order[p][0], toward[half])
+                        copy(d.at[blk, send], ra.at[half, p, send], s1, va.at[n], to).start()
+                    elif delta and delta != toward[half]:
+                        copy(d.at[blk, send], rb.at[half, p, send], s1, vb.at[n], peer(order[p][0], delta)).start()
+
+    joint = {}
+
+    def relay(b):
+        for p in range(PARTS):
+            for half in range(2):
+                with scope("wa"):
+                    incoming(ra, va, b, p, half)
+                blk = place(p, toward[half])
+                if b == 0:
+                    joint[p, half] = combine([d[blk, tile, :], ra[half, p, tile, :]])
+                    rd[half, p, tile, :] = joint[p, half][1]
+                c_own, c_far = joint[p, half][0]
+                rows = piece(b, half)
+                rd[half, p, rows, :] = c_own * d[blk, rows, :] + c_far * ra[half, p, rows, :]
+                rows, sem = parcel(b, half), vc.at[slot_of(b, p, half)]
+                copy(rd.at[half, p, rows], rc.at[half, p, rows], s1, sem, peer(order[p][0], toward[half])).start()
+
     factors = {}
-    for b in range(RING):
+
+    def gather(b):
         for p in range(PARTS):
-            with scope("w1"):
-                dst = r1.at[p, :, span(b)]
-                copy(dst, dst, s1, v1.at[b * PARTS + p], partner).wait_recv()
-            own = p * RING + first[p]
-            if b == 0:
-                factors[p] = combine([d[own, 0:STAT, :]] + [r1[p, i, 0:STAT, :] for i in range(3)])
-            scales, stats = factors[p]
-            total = scales[0] * d[own, body(b), :]
-            for i in range(3):
-                total = total + scales[i + 1] * r1[p, i, body(b), :]
-            e[p, b, 0:STAT, :] = stats
-            e[p, b, STAT:MSG2, :] = total
+            own = place(p, 0)
+            row = STAT
+            for half in range(2):
+                with scope("w1"):
+                    incoming(rb, vb, b, p, half)
+                    incoming(rc, vc, b, p, half)
+                if b == 0:
+                    factors[p, half] = combine([d[own, tile, :], rb[half, p, tile, :], rc[half, p, tile, :]])
+                c_own, c_one, c_two = factors[p, half][0]
+                rows = piece(b, half)
+                count = rows.stop - rows.start
+                e[p, b, row : row + count, :] = (
+                    c_own * d[own, rows, :] + c_one * rb[half, p, rows, :] + c_two * rc[half, p, rows, :]
+                )
+                row += count
+            e[p, b, 0:STAT, :] = factors[p, 0][1]
 
             @pl.when(mid[p] != b)
             def _():
                 delta = (b - mid[p] + RING) % RING
                 copy(e.at[p, b], r2.at[p, delta - 1], s2, v2.at[p], peer(order[p][1], delta)).start()
 
-        if b == 1:
-            link(1, unlink(0))
-        if b == 3:
-            link(2, unlink(1))
+    issue(2)
+    with scope("lm"):
+        head.wait()
+        both = lax.dot_general(q_ref[...], w_ref[...], (((1,), (1,)), ((), ())), preferred_element_type=F32)
+        mine = jnp.where(core == 0, both[:ROWS], both[ROWS:])
+        logits[...] = mine
+        lm_top = jnp.max(mine, axis=1, keepdims=True)
+        lm_sum = jnp.sum(jnp.exp(mine - lm_top), axis=1, keepdims=True)
+        lane = lax.broadcasted_iota(jnp.int32, (ROWS, LANES), 1)
+        pair = jnp.where(lane == 0, lm_top, lm_sum)
+        pair = jnp.concatenate([pair] * GROUPS, axis=0).T
+        link(0, pair[0:8, :])
+    for delta in (1, 3, 0):
+        issue(delta)
+    for b in range(RING):
+        relay(b)
+    link(1, unlink(0))
+    for b in range(RING):
+        gather(b)
+    link(2, unlink(1))
 
     for p in range(PARTS):
         with scope("w2"):
@@ -320,7 +372,9 @@
         lm = jnp.exp(logits[...] - turned[0:ROWS, 0:1]) / turned[0:ROWS, 1:2]
         logits[...] = (1.0 - mix) * lm
         copy(loc.at[1 - core], din, s0, v0.at[0], partner).wait_send()
-        copy(r1, r1, s1, v1.at[0], partner).wait_send()
+        for sent in (ra, rb, rc):
+            ref = sent.at[:, :, 0 : STAT + BLOCK // 2]
+            copy(ref, ref, s1, va.at[0], partner).wait_send()
         copy(r2, r2, s2, v2.at[0], partner).wait_send()
         copy(lr, lr, sl, vl.at[0], partner).wait_send()
 
@@ -384,7 +438,10 @@
                 pltpu.VMEM((2, PARTS * RING, MSG, LANES), F32),
                 pltpu.VMEM((PARTS * RING, MSG, LANES), F32),
                 pltpu.VMEM((PARTS * RING, MSG, LANES), F32),
-                pltpu.VMEM((PARTS, RING - 1, MSG, LANES), F32),
+                pltpu.VMEM((2, PARTS, MSG, LANES), F32),
+                pltpu.VMEM((2, PARTS, MSG, LANES), F32),
+                pltpu.VMEM((2, PARTS, MSG, LANES), F32),
+                pltpu.VMEM((2, PARTS, MSG, LANES), F32),
                 pltpu.VMEM((PARTS, RING, MSG2, LANES), F32),
                 pltpu.VMEM((PARTS, RING - 1, MSG2, LANES), F32),
                 pltpu.VMEM((PARTS, RING, MSG3, LANES), F32),
@@ -397,7 +454,9 @@
                 pltpu.SemaphoreType.DMA,
                 pltpu.SemaphoreType.DMA((12,)),
                 pltpu.SemaphoreType.DMA,
-                pltpu.SemaphoreType.DMA((12,)),
+                pltpu.SemaphoreType.DMA((24,)),
+                pltpu.SemaphoreType.DMA((24,)),
+                pltpu.SemaphoreType.DMA((24,)),
             ]
             + [pltpu.SemaphoreType.DMA, pltpu.SemaphoreType.DMA((3,))] * 3,
             compiler_params=pltpu.CompilerParams(collective_id=0, has_side_effects=True, vmem_limit_bytes=KB_LIMIT * 2**20),

time: 36.9 us -> 35.9 us (0.973)
  the two profiles are of different devices: /device:TPU:6 before, /device:TPU:1 now
where the time goes in v5:
time: 35.9 us; the launch traced here: 35.8 us
  Pallas kernels  33.9 us (94%)
  between operations  1.33 us (4%)
  local copies, waits for them, and re-layouts  0.62 us (2%)
    pallas_call x1, Pallas kernels, local_step(): pl.pallas_call(comm_kernel, out_shape=jax.ShapeDtypeStruct((ROWS, vocab_l...  24.6 us
    pallas_call x1, Pallas kernels, local_step(): pl.pallas_call(functools.partial(local_kernel, vocab_loc), out_shape=[jax...  9.23 us

profile of v5, /device:TPU:1, one launch (start us, length us, event | category | flops | bytes accessed | tf_op | source)
XLA Modules:
  0.0 35.8 jit_solution(16301126599348077823)
XLA Ops:
  1.3 0.0 copy-start
  1.3 9.2 %histogram.1 = (f32[6912,128]{1,0:T(8,128)S(1)}, f32[6912,128]{1,0:T(8,128)S(1)}, f32[6912,128]{1,0:T(8,128)S(1)}, f32[6912,128]{1,0:T(8,128)S(1)}, f32[8,256]{1,0:T(8,128)S(1)}) custom-call(f32[1,1]{1,0:T(1,128)} %bitcast.4.tau_ref, s32[16,128]{1,0:T(8,128)} %bitcast.7, bf16[16,2560]{1,0:T(8,128)(2,1)} %q_ref.1, bf16[2048,2560]{1,0:T(8,128)(2,1)} %k_hbm.1), custom_call_target="tpu_custom_call" | custom-call | tf_op jit(solution)/shard_map/histogram/pallas_call | solution.py:406
  10.5 0.0 copy-done
  10.6 24.6 %exchange.1 = f32[8,800]{1,0:T(8,128)S(1)} custom-call(f32[1,1]{1,0:T(1,128)} %bitcast.5.mix_ref, f32[6912,128]{1,0:T(8,128)S(1)} %get-tuple-element.10.h0, f32[6912,128]{1,0:T(8,128)S(1)} %get-tuple-element.11.h1, f32[6912,128]{1,0:T(8,128)S(1)} %get-tuple-element.12.h2, f32[6912,128]{1,0:T(8,128)S(1)} %get-tuple-element.13.h3, ...), custom_call_target="tpu_custom_call" | custom-call | tf_op jit(solution)/shard_map/exchange/pallas_call | solution.py:430
  35.2 0.6 %copy.10 = f32[8,800]{1,0:T(8,128)} copy(f32[8,800]{1,0:T(8,128)S(1)} %exchange.1) | data formatting | bytes 51200
Async XLA Ops:
  1.3 9.2 %copy-start = (bf16[16,2560]{1,0:T(8,128)(2,1)S(1)}, bf16[16,2560]{1,0:T(8,128)(2,1)}, u32[]{:S(2)}) copy-start(bf16[16,2560]{1,0:T(8,128)(2,1)} %q_ref.1) | copy-start | bytes 245764

commit v6 on v5

--- a/solution.py
+++ b/solution.py
@@ -18,15 +18,15 @@
 BLOCK = SLOTS * CHIPS // RING
 BLOCK2 = BLOCK // RING
 STAT = 8
-MSG = STAT + BLOCK
 MSG2 = STAT + BLOCK2
 MSG3 = 24
+NEAR = {1: 3, 3: 4, 0: 5}
 LEAD = 40
-HEAVY = 40
 NBUF = 4
 KA_LIMIT = 36
 KB_LIMIT = 36
-HROWS = 2 * SLOTS * CHIPS * PARTS
+HALF = SLOTS * CHIPS * PARTS + 8
+HROWS = 2 * HALF
 MESH = pl.DeviceIdType.MESH
 scope = jax.named_scope
 
@@ -41,6 +41,7 @@
     n_keys = k_ref.shape[0]
     quarter = n_keys // NBUF
     chunk = quarter // 2
+    part_rows = 64
 
     def fetch(j):
         rows = pl.ds(pl.multiple_of(j * chunk, chunk), chunk)
@@ -53,14 +54,14 @@
     for j in range(2):
         fetch(j).start()
     span = 288
-    pieces = HROWS // span // 3
+    pieces = 8
 
     for third in range(3):
 
         @pl.loop(third * pieces, (third + 1) * pieces)
         def _(i):
             for buf in hist:
-                buf[pl.ds(pl.multiple_of(i * span, 8), span), :] = jnp.zeros((span, LANES), F32)
+                buf[pl.ds(pl.multiple_of(i * span + (i // 12) * 8, 8), span), :] = jnp.zeros((span, LANES), F32)
 
         for j in range(2 + third * 2, 4 + third * 2):
             fetch(j).start()
@@ -80,7 +81,7 @@
         second = jnp.where(part == 0, y, jnp.where(part == 1, z, x))
         third = jnp.where(part == 0, z, jnp.where(part == 1, x, y))
         place = ((part * RING + first) * RING + second) * RING + third
-        idx[...] = (place * SLOTS + row) * 2
+        idx[...] = place * SLOTS + row
         put_idx = pltpu.make_async_copy(idx, idx_smem, isem)
         put_idx.start()
     with scope("mask"):
@@ -114,12 +115,17 @@
         with scope("dots"):
             keys = k_ref[pl.ds(pl.multiple_of(b * quarter, quarter), quarter), :]
             dots = jnp.dot(keys, qrep[...], preferred_element_type=F32)
-            kf = keys.astype(F32)
-            norms = jnp.sum(kf * kf, axis=1, keepdims=True)
-            scores = (2.0 * dots - norms) * inv
-            sc[...] = scores
-            top = jnp.max(scores.reshape(quarter // 8, 8, 2 * LANES), axis=0)
-            m = jnp.max(top, axis=0, keepdims=True)
+            tops = []
+            for r in range(0, quarter, part_rows):
+                squares = jnp.zeros((part_rows, LANES), F32)
+                for c in range(0, keys.shape[1], LANES):
+                    kf = keys[r : r + part_rows, c : c + LANES].astype(F32)
+                    squares = squares + kf * kf
+                norms = jnp.sum(squares, axis=1, keepdims=True)
+                scores = (2.0 * dots[r : r + part_rows] - norms) * inv
+                sc[r : r + part_rows, :] = scores
+                tops.append(jnp.max(scores.reshape(part_rows // 8, 8, 2 * LANES), axis=0))
+            m = jnp.max(functools.reduce(jnp.maximum, tops), axis=0, keepdims=True)
         with scope("expand"):
             total = jnp.zeros((8, 2 * LANES), F32)
             for c in range(quarter // LANES):
@@ -141,13 +147,14 @@
 
             @pl.loop(0, LANES // unroll)
             def _(i):
+                views = []
+                for b in range(NBUF):
+                    start = ((b * rows + c) * LANES + i * unroll) * 2
+                    views.append(wx.at[pl.ds(pl.multiple_of(start, 2 * unroll), 2 * unroll), :])
                 for u in range(unroll):
                     lane = i * unroll + u
-                    at = [pl.ds(pl.multiple_of(idx_smem[b * rows + c, lane], 2), 2) for b in range(NBUF)]
-                    new = [
-                        hist[b][at[b], :] + wx[pl.ds(pl.multiple_of(((b * rows + c) * LANES + lane) * 2, 2), 2), :]
-                        for b in range(NBUF)
-                    ]
+                    at = [pl.ds(idx_smem[b * rows + c, lane], 2, stride=HALF) for b in range(NBUF)]
+                    new = [hist[b][at[b], :] + views[b][2 * u : 2 * u + 2, :] for b in range(NBUF)]
                     for b in range(NBUF):
                         hist[b][at[b], :] = new[b]
 
@@ -155,7 +162,7 @@
 def comm_kernel(
     mix_ref, h0, h1, h2, h3, kstats, q_ref, w_hbm, out_ref,
     w_ref, logits, loc, din, d, ra, rb, rc, rd, e, r2, g3, r3, lt, lr, tsc, knn,
-    wsem, s0, v0, s1, va, vb, vc, s2, v2, s3, v3, sl, vl,
+    wsem, s0, v0, s1, va, vb, s2, v2, s3, v3, sl, vl,
 ):
     core = lax.axis_index("store")
     chip = lax.axis_index("model")
@@ -186,16 +193,16 @@
         @pl.loop(0, PARTS * RING)
         def _(blk):
             for h in range(2):
-                loc[h, blk, LEAD : LEAD + STAT, :] = jnp.concatenate(
-                    [top[:, half[h]], mass[:, half[h]], jnp.zeros((STAT - 2, LANES), F32)], axis=0
-                )
-                for t in range(BLOCK // 8):
-                    at = pl.ds(blk * 2 * BLOCK + t * 16 + h, 8, stride=2)
-                    total = scales[0][:, half[h]] * hist[0][at, :]
-                    for b in range(1, NBUF):
-                        total = total + scales[b][:, half[h]] * hist[b][at, :]
-                    row = t * 8 if t * 8 < LEAD else t * 8 + STAT
-                    loc[h, blk, row : row + 8, :] = total
+                stats = jnp.concatenate([top[:, half[h]], mass[:, half[h]], jnp.zeros((STAT - 2, LANES), F32)], axis=0)
+                for b in range(RING):
+                    loc[h, blk, b, LEAD : LEAD + STAT, :] = stats
+                    for t in range(BLOCK2 // 8):
+                        at = pl.ds(pl.multiple_of(h * HALF + blk * BLOCK + b * BLOCK2 + t * 8, 8), 8)
+                        total = scales[0][:, half[h]] * hist[0][at, :]
+                        for n in range(1, NBUF):
+                            total = total + scales[n][:, half[h]] * hist[n][at, :]
+                        row = t * 8 if t * 8 < LEAD else t * 8 + STAT
+                        loc[h, blk, b, row : row + 8, :] = total
 
     with scope("barrier"):
         pl.semaphore_wait(barrier, 10)
@@ -203,23 +210,17 @@
     def copy(src, dst, ssem, rsem, to):
         return pltpu.make_async_remote_copy(src_ref=src, dst_ref=dst, send_sem=ssem, recv_sem=rsem, device_id=to, device_id_type=MESH)
 
-    def span(b):
-        return slice(0, MSG2) if b == 0 else slice(STAT + b * BLOCK2, STAT + (b + 1) * BLOCK2)
-
-    def piece(b, half):
-        cut = HEAVY if b % 2 == 0 else BLOCK2 - HEAVY
-        start = STAT + b * BLOCK2
-        if b == 0:
-            return slice(0, LEAD) if half == 0 else slice(LEAD + STAT, MSG2)
-        return slice(start, start + cut) if half == 0 else slice(start + cut, start + BLOCK2)
-
-    def parcel(b, half):
-        if b == 0:
+    tile = slice(LEAD, LEAD + STAT)
+    pieces = (slice(0, LEAD), slice(LEAD + STAT, MSG2))
+    turn = (2, 1, 3, 0)
+    toward = (1, RING - 1)
+
+    def parcel(k, way):
+        half = (way + k) % 2
+        if k == 0:
             return slice(0, LEAD + STAT) if half == 0 else slice(LEAD, MSG2)
-        return piece(b, half)
-
-    tile = slice(LEAD, LEAD + STAT)
-    toward = (1, RING - 1)
+        return pieces[half]
+
     partner = {"store": 1 - core}
     first = [dims[order[p][0]][0] for p in range(PARTS)]
     mid = [dims[order[p][1]][0] for p in range(PARTS)]
@@ -230,18 +231,14 @@
 
     def near(p, delta):
         blk = place(p, delta)
-        return copy(loc.at[1 - core, blk], din.at[blk], s0, v0.at[p * RING + delta], partner)
+        return copy(loc.at[1 - core, blk], din.at[blk], s0, v0.at[p if delta == 2 else NEAR[delta]], partner)
 
     for delta in (2, 1, 3, 0):
         for p in range(PARTS):
             near(p, delta).start()
 
-    def slot_of(b, p, half):
-        return (b * PARTS + p) * 2 + half
-
-    def incoming(dst, sem, b, p, half):
-        ref = dst.at[half, p, parcel(b, half)]
-        copy(ref, ref, s1, sem.at[slot_of(b, p, half)], partner).wait_recv()
+    def arrived(ref, sem, ssem=s1):
+        copy(ref, ref, ssem, sem, partner).wait_recv()
 
     def link(axis, tile):
         lt[axis] = tile
@@ -267,64 +264,63 @@
         for p in range(PARTS):
             blk = place(p, delta)
             with scope("w0"):
-                near(p, delta).wait_recv()
+                if delta == 2:
+                    near(p, delta).wait_recv()
+                elif p == 0:
+                    arrived(din.at[0:PARTS], v0.at[NEAR[delta]], s0)
             if not chipwise:
-                chipwise.append(combine([loc[core, 0, tile, :], din[blk, tile, :]]))
+                chipwise.append(combine([loc[core, 0, 0, tile, :], din[blk, 0, tile, :]]))
             (c_own, c_par), stats = chipwise[0]
-            d[blk, tile, :] = stats
-            for b in range(RING):
-                for half in range(2):
-                    rows = piece(b, half)
-                    d[blk, rows, :] = c_own * loc[core, blk, rows, :] + c_par * din[blk, rows, :]
-                    n, send = slot_of(b, p, half), parcel(b, half)
+            for k in range(RING):
+                b = (mid[p] + turn[k]) % RING
+                if k == 0:
+                    d[p, delta, k, tile, :] = stats
+                for rows in pieces:
+                    d[p, delta, k, rows, :] = c_own * loc[core, blk, b, rows, :] + c_par * din[blk, b, rows, :]
+                for way in range(2):
+                    rows = parcel(k, way)
                     if delta == 2:
-                        to = peer(order[p][0], toward[half])
-                        copy(d.at[blk, send], ra.at[half, p, send], s1, va.at[n], to).start()
-                    elif delta and delta != toward[half]:
-                        copy(d.at[blk, send], rb.at[half, p, send], s1, vb.at[n], peer(order[p][0], delta)).start()
+                        to = peer(order[p][0], toward[way])
+                        copy(d.at[p, delta, k, rows], ra.at[way, p, k, rows], s1, va.at[k], to).start()
+                    elif delta == toward[1 - way]:
+                        to = peer(order[p][0], delta)
+                        copy(d.at[p, delta, k, rows], rb.at[way, p, k, rows], s1, vb.at[k * PARTS + p], to).start()
 
     joint = {}
 
-    def relay(b):
+    def relay(k):
+        with scope("wa"):
+            arrived(din.at[0:11, 0, 0:24] if k == 0 else ra.at[0, :, k, 0:BLOCK2], va.at[k])
         for p in range(PARTS):
-            for half in range(2):
-                with scope("wa"):
-                    incoming(ra, va, b, p, half)
-                blk = place(p, toward[half])
-                if b == 0:
-                    joint[p, half] = combine([d[blk, tile, :], ra[half, p, tile, :]])
-                    rd[half, p, tile, :] = joint[p, half][1]
-                c_own, c_far = joint[p, half][0]
-                rows = piece(b, half)
-                rd[half, p, rows, :] = c_own * d[blk, rows, :] + c_far * ra[half, p, rows, :]
-                rows, sem = parcel(b, half), vc.at[slot_of(b, p, half)]
-                copy(rd.at[half, p, rows], rc.at[half, p, rows], s1, sem, peer(order[p][0], toward[half])).start()
+            for way in range(2):
+                if k == 0:
+                    joint[p, way] = combine([d[p, toward[way], k, tile, :], ra[way, p, k, tile, :]])
+                    rd[way, p, k, tile, :] = joint[p, way][1]
+                c_own, c_far = joint[p, way][0]
+                rows = pieces[(way + k) % 2]
+                rd[way, p, k, rows, :] = c_own * d[p, toward[way], k, rows, :] + c_far * ra[way, p, k, rows, :]
+                rows = parcel(k, way)
+                to = peer(order[p][0], toward[way])
+                copy(rd.at[way, p, k, rows], rc.at[way, p, k, rows], s1, vb.at[k * PARTS + p], to).start()
 
     factors = {}
 
-    def gather(b):
+    def gather(k):
         for p in range(PARTS):
-            own = place(p, 0)
-            row = STAT
-            for half in range(2):
-                with scope("w1"):
-                    incoming(rb, vb, b, p, half)
-                    incoming(rc, vc, b, p, half)
-                if b == 0:
-                    factors[p, half] = combine([d[own, tile, :], rb[half, p, tile, :], rc[half, p, tile, :]])
-                c_own, c_one, c_two = factors[p, half][0]
-                rows = piece(b, half)
-                count = rows.stop - rows.start
-                e[p, b, row : row + count, :] = (
-                    c_own * d[own, rows, :] + c_one * rb[half, p, rows, :] + c_two * rc[half, p, rows, :]
+            with scope("w1"):
+                arrived(din.at[0:11, 0, 0:16] if k == 0 else din.at[0:2, 0, 0:BLOCK2], vb.at[k * PARTS + p])
+            for way in range(2):
+                if k == 0:
+                    factors[p, way] = combine([d[p, 0, k, tile, :], rb[way, p, k, tile, :], rc[way, p, k, tile, :]])
+                c_own, c_one, c_two = factors[p, way][0]
+                rows = pieces[(way + k) % 2]
+                at = STAT + (rows.start if rows.start == 0 else LEAD)
+                e[p, k, at : at + rows.stop - rows.start, :] = (
+                    c_own * d[p, 0, k, rows, :] + c_one * rb[way, p, k, rows, :] + c_two * rc[way, p, k, rows, :]
                 )
-                row += count
-            e[p, b, 0:STAT, :] = factors[p, 0][1]
-
-            @pl.when(mid[p] != b)
-            def _():
-                delta = (b - mid[p] + RING) % RING
-                copy(e.at[p, b], r2.at[p, delta - 1], s2, v2.at[p], peer(order[p][1], delta)).start()
+            e[p, k, 0:STAT, :] = factors[p, 0][1]
+            if turn[k]:
+                copy(e.at[p, k], r2.at[p, turn[k] - 1], s2, v2.at[p], peer(order[p][1], turn[k])).start()
 
     issue(2)
     with scope("lm"):
@@ -350,11 +346,10 @@
     for p in range(PARTS):
         with scope("w2"):
             copy(r2.at[p], r2.at[p], s2, v2.at[p], partner).wait_recv()
-        own = mid[p]
-        scales, stats = combine([e[p, own, 0:STAT, :]] + [r2[p, i, 0:STAT, :] for i in range(3)])
+        scales, stats = combine([e[p, 3, 0:STAT, :]] + [r2[p, i, 0:STAT, :] for i in range(3)])
         for c in range(RING):
             rows = slice(STAT + c * SLOTS, STAT + (c + 1) * SLOTS)
-            total = scales[0] * e[p, own, rows, :]
+            total = scales[0] * e[p, 3, rows, :]
             for i in range(3):
                 total = total + scales[i + 1] * r2[p, i, rows, :]
             g3[p, c, 0:SLOTS, :] = total
@@ -373,8 +368,8 @@
         logits[...] = (1.0 - mix) * lm
         copy(loc.at[1 - core], din, s0, v0.at[0], partner).wait_send()
         for sent in (ra, rb, rc):
-            ref = sent.at[:, :, 0 : STAT + BLOCK // 2]
-            copy(ref, ref, s1, va.at[0], partner).wait_send()
+            for ref in (din.at[0:11, 0, 0:24], sent.at[0, :, 1:RING, 0:BLOCK2]):
+                copy(ref, ref, s1, va.at[0], partner).wait_send()
         copy(r2, r2, s2, v2.at[0], partner).wait_send()
         copy(lr, lr, sl, vl.at[0], partner).wait_send()
 
@@ -435,13 +430,13 @@
             scratch_shapes=[
                 pltpu.VMEM(w_head.shape[::-1], jnp.bfloat16),
                 pltpu.VMEM((ROWS, vocab_loc), F32),
-                pltpu.VMEM((2, PARTS * RING, MSG, LANES), F32),
-                pltpu.VMEM((PARTS * RING, MSG, LANES), F32),
-                pltpu.VMEM((PARTS * RING, MSG, LANES), F32),
-                pltpu.VMEM((2, PARTS, MSG, LANES), F32),
-                pltpu.VMEM((2, PARTS, MSG, LANES), F32),
-                pltpu.VMEM((2, PARTS, MSG, LANES), F32),
-                pltpu.VMEM((2, PARTS, MSG, LANES), F32),
+                pltpu.VMEM((2, PARTS * RING, RING, MSG2, LANES), F32),
+                pltpu.VMEM((PARTS * RING, RING, MSG2, LANES), F32),
+                pltpu.VMEM((PARTS, RING, RING, MSG2, LANES), F32),
+                pltpu.VMEM((2, PARTS, RING, MSG2, LANES), F32),
+                pltpu.VMEM((2, PARTS, RING, MSG2, LANES), F32),
+                pltpu.VMEM((2, PARTS, RING, MSG2, LANES), F32),
+                pltpu.VMEM((2, PARTS, RING, MSG2, LANES), F32),
                 pltpu.VMEM((PARTS, RING, MSG2, LANES), F32),
                 pltpu.VMEM((PARTS, RING - 1, MSG2, LANES), F32),
                 pltpu.VMEM((PARTS, RING, MSG3, LANES), F32),
@@ -452,11 +447,10 @@
                 pltpu.VMEM((ROWS, vocab_loc), F32),
                 pltpu.SemaphoreType.DMA,
                 pltpu.SemaphoreType.DMA,
+                pltpu.SemaphoreType.DMA((6,)),
+                pltpu.SemaphoreType.DMA,
+                pltpu.SemaphoreType.DMA((4,)),
                 pltpu.SemaphoreType.DMA((12,)),
-                pltpu.SemaphoreType.DMA,
-                pltpu.SemaphoreType.DMA((24,)),
-                pltpu.SemaphoreType.DMA((24,)),
-                pltpu.SemaphoreType.DMA((24,)),
             ]
             + [pltpu.SemaphoreType.DMA, pltpu.SemaphoreType.DMA((3,))] * 3,
             compiler_params=pltpu.CompilerParams(collective_id=0, has_side_effects=True, vmem_limit_bytes=KB_LIMIT * 2**20),

time: 35.9 us -> 35.1 us (0.978)
  Pallas kernels: 33.9 us -> 33 us
    pallas_call x1, Pallas kernels: 24.6 us -> 23.7 us  [local_step(): pl.pallas_call(comm_kernel, out_shape=jax.ShapeDtypeStruct((ROWS, vocab_l...]
where the time goes in v6:
time: 35.1 us; the launch traced here: 35 us
  Pallas kernels  33 us (94%)
  between operations  1.33 us (4%)
  local copies, waits for them, and re-layouts  0.62 us (2%)
    pallas_call x1, Pallas kernels, local_step(): pl.pallas_call(comm_kernel, out_shape=jax.ShapeDtypeStruct((ROWS, vocab_l...  23.7 us
    pallas_call x1, Pallas kernels, local_step(): pl.pallas_call(functools.partial(local_kernel, vocab_loc), out_shape=[jax...  9.33 us

profile of v6, /device:TPU:1, one launch (start us, length us, event | category | flops | bytes accessed | tf_op | source)
XLA Modules:
  0.0 35.0 jit_solution(1690190114160887943)
XLA Ops:
  1.3 0.0 copy-start
  1.3 9.3 %histogram.1 = (f32[6928,128]{1,0:T(8,128)S(1)}, f32[6928,128]{1,0:T(8,128)S(1)}, f32[6928,128]{1,0:T(8,128)S(1)}, f32[6928,128]{1,0:T(8,128)S(1)}, f32[8,256]{1,0:T(8,128)S(1)}) custom-call(f32[1,1]{1,0:T(1,128)} %bitcast.4.tau_ref, s32[16,128]{1,0:T(8,128)} %bitcast.7, bf16[16,2560]{1,0:T(8,128)(2,1)} %q_ref.1, bf16[2048,2560]{1,0:T(8,128)(2,1)} %k_hbm.1), custom_call_target="tpu_custom_call" | custom-call | tf_op jit(solution)/shard_map/histogram/pallas_call | solution.py:401
  10.6 0.0 copy-done
  10.7 23.7 %exchange.1 = f32[8,800]{1,0:T(8,128)S(1)} custom-call(f32[1,1]{1,0:T(1,128)} %bitcast.5.mix_ref, f32[6928,128]{1,0:T(8,128)S(1)} %get-tuple-element.10.h0, f32[6928,128]{1,0:T(8,128)S(1)} %get-tuple-element.11.h1, f32[6928,128]{1,0:T(8,128)S(1)} %get-tuple-element.12.h2, f32[6928,128]{1,0:T(8,128)S(1)} %get-tuple-element.13.h3, ...), custom_call_target="tpu_custom_call" | custom-call | tf_op jit(solution)/shard_map/exchange/pallas_call | solution.py:425
  34.4 0.6 %copy.10 = f32[8,800]{1,0:T(8,128)} copy(f32[8,800]{1,0:T(8,128)S(1)} %exchange.1) | data formatting | bytes 51200
Async XLA Ops:
  1.3 9.4 %copy-start = (bf16[16,2560]{1,0:T(8,128)(2,1)S(1)}, bf16[16,2560]{1,0:T(8,128)(2,1)}, u32[]{:S(2)}) copy-start(bf16[16,2560]{1,0:T(8,128)(2,1)} %q_ref.1) | copy-start | bytes 245764

commit v7 on v6

--- a/solution.py
+++ b/solution.py
@@ -63,7 +63,7 @@
             for buf in hist:
                 buf[pl.ds(pl.multiple_of(i * span + (i // 12) * 8, 8), span), :] = jnp.zeros((span, LANES), F32)
 
-        for j in range(2 + third * 2, 4 + third * 2):
+        for j in ((), (2, 3), (4, 5, 6, 7))[third]:
             fetch(j).start()
 
     get_tok.wait()
@@ -81,11 +81,14 @@
         second = jnp.where(part == 0, y, jnp.where(part == 1, z, x))
         third = jnp.where(part == 0, z, jnp.where(part == 1, x, y))
         place = ((part * RING + first) * RING + second) * RING + third
-        idx[...] = place * SLOTS + row
-        put_idx = pltpu.make_async_copy(idx, idx_smem, isem)
-        put_idx.start()
+        place = place * SLOTS + row
+        idx[...] = place
+        for r in range(n_keys // LANES):
+            pltpu.make_async_copy(idx.at[r], idx_smem.at[pl.ds(r * LANES, LANES)], isem).start()
+        lane = lax.broadcasted_iota(jnp.int32, place.shape, 1)
+        again = jnp.logical_and(place == pltpu.roll(place, 1, 1), lane % 2 == 1)
     with scope("mask"):
-        group = group.astype(F32)
+        group = group.astype(F32) + jnp.where(again, float(GROUPS), 0.0)
         square = (LANES, LANES)
         eye = lax.broadcasted_iota(jnp.int32, square, 0) == lax.broadcasted_iota(jnp.int32, square, 1)
         ones = jnp.ones(square, jnp.bfloat16)
@@ -95,14 +98,11 @@
 
     with scope("turn"):
         get_q.wait()
-        pick = (2 * ROWS, 2 * LANES)
-        lane = lax.broadcasted_iota(jnp.int32, pick, 1)
-        pick = lax.broadcasted_iota(jnp.int32, pick, 0) == (lane // LANES) * ROWS + lane % ROWS
-        pick = pick.astype(F32).astype(jnp.bfloat16)
-        wide = 512
-        for c in range(0, q_ref.shape[1], wide):
-            turned = lax.dot_general(q_ref[:, c : c + wide], pick, (((0,), (0,)), ((), ())), preferred_element_type=F32)
-            qrep[c : c + wide, :] = turned.astype(jnp.bfloat16)
+        for h in range(2):
+            half = q_ref[h * ROWS : (h + 1) * ROWS, :].astype(F32)
+            pair = jnp.concatenate([half, half], axis=0).astype(jnp.bfloat16)
+            for g in range(GROUPS // 2):
+                qrep[pl.ds(h * LANES + g * 2 * ROWS, 2 * ROWS), :] = pair
 
     inv = 1.0 / tau_ref[0, 0]
     lane_group = (lax.broadcasted_iota(jnp.int32, (LANES, LANES), 1) // ROWS).astype(F32)
@@ -114,7 +114,7 @@
                 fetch(b * 2 + sub).wait()
         with scope("dots"):
             keys = k_ref[pl.ds(pl.multiple_of(b * quarter, quarter), quarter), :]
-            dots = jnp.dot(keys, qrep[...], preferred_element_type=F32)
+            dots = lax.dot_general(keys, qrep[...], (((1,), (1,)), ((), ())), preferred_element_type=F32)
             tops = []
             for r in range(0, quarter, part_rows):
                 squares = jnp.zeros((part_rows, LANES), F32)
@@ -132,14 +132,18 @@
                 w = jnp.exp(sc[c * LANES : (c + 1) * LANES, :] - m)
                 total = total + jnp.sum(w.reshape(LANES // 8, 8, 2 * LANES), axis=0)
                 at = b * quarter + c * LANES
-                mine = grp[pl.ds(pl.multiple_of(at, LANES), LANES), :] == lane_group
+                tag = grp[pl.ds(pl.multiple_of(at, LANES), LANES), :]
+                repeat = tag >= GROUPS
+                mine = jnp.where(repeat, tag - GROUPS, tag) == lane_group
                 for h in range(2):
-                    wx[pl.ds(at * 2 + h, LANES, stride=2), :] = jnp.where(mine, w[:, h * LANES : (h + 1) * LANES], 0.0)
+                    own = jnp.where(mine, w[:, h * LANES : (h + 1) * LANES], 0.0)
+                    before = pltpu.roll(own.reshape(LANES // 8, 8, LANES), 1, 1).reshape(LANES, LANES)
+                    wx[pl.ds(at * 2 + h, LANES, stride=2), :] = own + jnp.where(repeat, before, 0.0)
             total = jnp.sum(total, axis=0, keepdims=True)
             stats_ref[pl.ds(b, 1), :] = m
             stats_ref[pl.ds(NBUF + b, 1), :] = total
 
-    put_idx.wait()
+    pltpu.make_async_copy(idx, tok_ref, isem).wait()
     unroll = 8
     rows = quarter // LANES
     with scope("scatter"):
@@ -151,18 +155,19 @@
                 for b in range(NBUF):
                     start = ((b * rows + c) * LANES + i * unroll) * 2
                     views.append(wx.at[pl.ds(pl.multiple_of(start, 2 * unroll), 2 * unroll), :])
-                for u in range(unroll):
-                    lane = i * unroll + u
-                    at = [pl.ds(idx_smem[b * rows + c, lane], 2, stride=HALF) for b in range(NBUF)]
-                    new = [hist[b][at[b], :] + views[b][2 * u : 2 * u + 2, :] for b in range(NBUF)]
-                    for b in range(NBUF):
-                        hist[b][at[b], :] = new[b]
+                for u in range(0, unroll, 2):
+                    both = [(b, v) for b in range(NBUF) for v in (u, u + 1)]
+                    at = [idx_smem[(b * rows + c) * LANES + i * unroll + v] for b, v in both]
+                    at = [pl.ds(row, 2, stride=HALF) for row in at]
+                    new = [hist[b][at[n], :] + views[b][2 * v : 2 * v + 2, :] for n, (b, v) in enumerate(both)]
+                    for n, (b, v) in enumerate(both):
+                        hist[b][at[n], :] = new[n]
 
 
 def comm_kernel(
     mix_ref, h0, h1, h2, h3, kstats, q_ref, w_hbm, out_ref,
     w_ref, logits, loc, din, d, ra, rb, rc, rd, e, r2, g3, r3, lt, lr, tsc, knn,
-    wsem, s0, v0, s1, va, vb, s2, v2, s3, v3, sl, vl,
+    wsem, s0, v0, s1, va, vb, ready, s2, v2, s3, v3, sl, vl,
 ):
     core = lax.axis_index("store")
     chip = lax.axis_index("model")
@@ -176,9 +181,9 @@
 
     barrier = pltpu.get_barrier_semaphore()
     pl.semaphore_signal(barrier, inc=1, device_id={"store": 1 - core}, device_id_type=MESH)
-    for axis in range(3):
-        for delta in range(1, RING):
-            pl.semaphore_signal(barrier, inc=1, device_id=peer(axis, delta), device_id_type=MESH)
+    beside = [peer(axis, delta) for axis in range(3) for delta in (1, RING - 1)]
+    for to in beside:
+        pl.semaphore_signal(barrier, inc=1, device_id=to, device_id_type=MESH)
     head = pltpu.make_async_copy(w_hbm, w_ref, wsem)
     head.start()
 
@@ -188,24 +193,29 @@
     mass = sum(c * kstats[NBUF + b : NBUF + b + 1, :] for b, c in enumerate(scales))
     half = [slice(h * LANES, (h + 1) * LANES) for h in range(2)]
 
+    def add_up(j):
+        turn, p = j // PARTS, j % PARTS
+        delta = jnp.where(turn == 0, 2, jnp.where(turn == 1, 1, jnp.where(turn == 2, 3, 0)))
+        blk = p * RING + ((chip >> (2 * p)) + delta) % RING
+        for h in range(2):
+            stats = jnp.concatenate([top[:, half[h]], mass[:, half[h]], jnp.zeros((STAT - 2, LANES), F32)], axis=0)
+            for b in range(RING):
+                loc[h, blk, b, LEAD : LEAD + STAT, :] = stats
+                for t in range(BLOCK2 // 8):
+                    at = pl.ds(pl.multiple_of(h * HALF + blk * BLOCK + b * BLOCK2 + t * 8, 8), 8)
+                    total = scales[0][:, half[h]] * hist[0][at, :]
+                    for n in range(1, NBUF):
+                        total = total + scales[n][:, half[h]] * hist[n][at, :]
+                    row = t * 8 if t * 8 < LEAD else t * 8 + STAT
+                    loc[h, blk, b, row : row + 8, :] = total
+
     with scope("sum"):
-
-        @pl.loop(0, PARTS * RING)
-        def _(blk):
-            for h in range(2):
-                stats = jnp.concatenate([top[:, half[h]], mass[:, half[h]], jnp.zeros((STAT - 2, LANES), F32)], axis=0)
-                for b in range(RING):
-                    loc[h, blk, b, LEAD : LEAD + STAT, :] = stats
-                    for t in range(BLOCK2 // 8):
-                        at = pl.ds(pl.multiple_of(h * HALF + blk * BLOCK + b * BLOCK2 + t * 8, 8), 8)
-                        total = scales[0][:, half[h]] * hist[0][at, :]
-                        for n in range(1, NBUF):
-                            total = total + scales[n][:, half[h]] * hist[n][at, :]
-                        row = t * 8 if t * 8 < LEAD else t * 8 + STAT
-                        loc[h, blk, b, row : row + 8, :] = total
+        pl.loop(0, PARTS)(add_up)
 
     with scope("barrier"):
-        pl.semaphore_wait(barrier, 10)
+        pl.semaphore_wait(barrier, 7)
+    for to in beside:
+        pl.semaphore_signal(ready, inc=1, device_id=to, device_id_type=MESH)
 
     def copy(src, dst, ssem, rsem, to):
         return pltpu.make_async_remote_copy(src_ref=src, dst_ref=dst, send_sem=ssem, recv_sem=rsem, device_id=to, device_id_type=MESH)
@@ -233,7 +243,11 @@
         blk = place(p, delta)
         return copy(loc.at[1 - core, blk], din.at[blk], s0, v0.at[p if delta == 2 else NEAR[delta]], partner)
 
-    for delta in (2, 1, 3, 0):
+    for p in range(PARTS):
+        near(p, 2).start()
+    with scope("sum2"):
+        pl.loop(PARTS, PARTS * RING)(add_up)
+    for delta in (1, 3, 0):
         for p in range(PARTS):
             near(p, delta).start()
 
@@ -333,6 +347,7 @@
         lane = lax.broadcasted_iota(jnp.int32, (ROWS, LANES), 1)
         pair = jnp.where(lane == 0, lm_top, lm_sum)
         pair = jnp.concatenate([pair] * GROUPS, axis=0).T
+        pl.semaphore_wait(ready, 6)
         link(0, pair[0:8, :])
     for delta in (1, 3, 0):
         issue(delta)
@@ -406,12 +421,12 @@
             scratch_shapes=[
                 pltpu.VMEM(queries.shape, jnp.bfloat16),
                 pltpu.VMEM(store_keys.shape, jnp.bfloat16),
-                pltpu.VMEM((width, 2 * LANES), jnp.bfloat16),
+                pltpu.VMEM((2 * LANES, width), jnp.bfloat16),
                 pltpu.VMEM((n_keys // NBUF, 2 * LANES), F32),
                 pltpu.VMEM((2 * n_keys, LANES), F32),
                 pltpu.VMEM((n_keys, LANES), F32),
                 pltpu.VMEM((n_keys // LANES, LANES), jnp.int32),
-                pltpu.SMEM((n_keys // LANES, LANES), jnp.int32),
+                pltpu.SMEM((n_keys,), jnp.int32),
                 pltpu.VMEM((n_keys // LANES, LANES), jnp.int32),
                 pltpu.SemaphoreType.DMA,
                 pltpu.SemaphoreType.DMA,
@@ -451,6 +466,7 @@
                 pltpu.SemaphoreType.DMA,
                 pltpu.SemaphoreType.DMA((4,)),
                 pltpu.SemaphoreType.DMA((12,)),
+                pltpu.SemaphoreType.REGULAR,
             ]
             + [pltpu.SemaphoreType.DMA, pltpu.SemaphoreType.DMA((3,))] * 3,
             compiler_params=pltpu.CompilerParams(collective_id=0, has_side_effects=True, vmem_limit_bytes=KB_LIMIT * 2**20),

time: 35.1 us -> 34.1 us (0.972); the launches traced: 35 us -> 33.5 us
  Pallas kernels: 33 us -> 31.5 us
    pallas_call x1, Pallas kernels: 9.33 us -> 8.38 us  [local_step(): pl.pallas_call(functools.partial(local_kernel, vocab_loc), out_shape=[jax...]
    pallas_call x1, Pallas kernels: 23.7 us -> 23.1 us  [local_step(): pl.pallas_call(comm_kernel, out_shape=jax.ShapeDtypeStruct((ROWS, vocab_l...]
where the time goes in v7:
time: 34.1 us; the launch traced here: 33.5 us
  Pallas kernels  31.5 us (92%)
  between operations  1.33 us (4%)
  local copies, waits for them, and re-layouts  0.62 us (2%)
    pallas_call x1, Pallas kernels, local_step(): pl.pallas_call(comm_kernel, out_shape=jax.ShapeDtypeStruct((ROWS, vocab_l...  23.1 us
    pallas_call x1, Pallas kernels, local_step(): pl.pallas_call(functools.partial(local_kernel, vocab_loc), out_shape=[jax...  8.38 us

profile of v7, /device:TPU:1, one launch (start us, length us, event | category | flops | bytes accessed | tf_op | source)
XLA Modules:
  0.0 33.5 jit_solution(6607537125969714447)
XLA Ops:
  1.3 0.0 copy-start
  1.3 8.4 %histogram.1 = (f32[6928,128]{1,0:T(8,128)S(1)}, f32[6928,128]{1,0:T(8,128)S(1)}, f32[6928,128]{1,0:T(8,128)S(1)}, f32[6928,128]{1,0:T(8,128)S(1)}, f32[8,256]{1,0:T(8,128)S(1)}) custom-call(f32[1,1]{1,0:T(1,128)} %bitcast.4.tau_ref, s32[16,128]{1,0:T(8,128)} %bitcast.7, bf16[16,2560]{1,0:T(8,128)(2,1)} %q_ref.1, bf16[2048,2560]{1,0:T(8,128)(2,1)} %k_hbm.1), custom_call_target="tpu_custom_call" | custom-call | tf_op jit(solution)/shard_map/histogram/pallas_call | solution.py:416
  9.7 0.0 copy-done
  9.7 23.1 %exchange.1 = f32[8,800]{1,0:T(8,128)S(1)} custom-call(f32[1,1]{1,0:T(1,128)} %bitcast.5.mix_ref, f32[6928,128]{1,0:T(8,128)S(1)} %get-tuple-element.10.h0, f32[6928,128]{1,0:T(8,128)S(1)} %get-tuple-element.11.h1, f32[6928,128]{1,0:T(8,128)S(1)} %get-tuple-element.12.h2, f32[6928,128]{1,0:T(8,128)S(1)} %get-tuple-element.13.h3, ...), custom_call_target="tpu_custom_call" | custom-call | tf_op jit(solution)/shard_map/exchange/pallas_call | solution.py:440
  32.8 0.6 %copy.10 = f32[8,800]{1,0:T(8,128)} copy(f32[8,800]{1,0:T(8,128)S(1)} %exchange.1) | data formatting | bytes 51200
Async XLA Ops:
  1.3 8.4 %copy-start = (bf16[16,2560]{1,0:T(8,128)(2,1)S(1)}, bf16[16,2560]{1,0:T(8,128)(2,1)}, u32[]{:S(2)}) copy-start(bf16[16,2560]{1,0:T(8,128)(2,1)} %q_ref.1) | copy-start | bytes 245764

commit v8 on v7

--- a/solution.py
+++ b/solution.py
@@ -167,7 +167,7 @@
 def comm_kernel(
     mix_ref, h0, h1, h2, h3, kstats, q_ref, w_hbm, out_ref,
     w_ref, logits, loc, din, d, ra, rb, rc, rd, e, r2, g3, r3, lt, lr, tsc, knn,
-    wsem, s0, v0, s1, va, vb, ready, s2, v2, s3, v3, sl, vl,
+    wsem, s0, v0, s1, va, vb, ready, pal, s2, v2, s3, v3, sl, vl,
 ):
     core = lax.axis_index("store")
     chip = lax.axis_index("model")
@@ -180,12 +180,21 @@
         return {"model": chip + ((at + delta) % RING - at) * stride}
 
     barrier = pltpu.get_barrier_semaphore()
-    pl.semaphore_signal(barrier, inc=1, device_id={"store": 1 - core}, device_id_type=MESH)
     beside = [peer(axis, delta) for axis in range(3) for delta in (1, RING - 1)]
     for to in beside:
-        pl.semaphore_signal(barrier, inc=1, device_id=to, device_id_type=MESH)
+        pl.semaphore_signal(barrier, inc=1, device_id={**to, "store": 1}, device_id_type=MESH)
+
+    @pl.when(core == 1)
+    def _():
+        pl.semaphore_signal(barrier, inc=1, device_id={"store": 0}, device_id_type=MESH)
+
     head = pltpu.make_async_copy(w_hbm, w_ref, wsem)
     head.start()
+
+    @pl.when(core == 0)
+    def _():
+        pl.semaphore_wait(barrier, 1)
+        pl.semaphore_signal(pal, inc=1, device_id={"store": 1}, device_id_type=MESH)
 
     hist = (h0, h1, h2, h3)
     top = functools.reduce(jnp.maximum, [kstats[b : b + 1, :] for b in range(NBUF)])
@@ -212,10 +221,9 @@
     with scope("sum"):
         pl.loop(0, PARTS)(add_up)
 
-    with scope("barrier"):
-        pl.semaphore_wait(barrier, 7)
-    for to in beside:
-        pl.semaphore_signal(ready, inc=1, device_id=to, device_id_type=MESH)
+    @pl.when(core == 1)
+    def _():
+        pl.semaphore_wait(pal, 1)
 
     def copy(src, dst, ssem, rsem, to):
         return pltpu.make_async_remote_copy(src_ref=src, dst_ref=dst, send_sem=ssem, recv_sem=rsem, device_id=to, device_id_type=MESH)
@@ -232,6 +240,10 @@
         return pieces[half]
 
     partner = {"store": 1 - core}
+
+    def across(axis, delta):
+        return {**peer(axis, delta), "store": 1 - core} if delta else partner
+
     first = [dims[order[p][0]][0] for p in range(PARTS)]
     mid = [dims[order[p][1]][0] for p in range(PARTS)]
     last = [dims[order[p][2]][0] for p in range(PARTS)]
@@ -250,6 +262,20 @@
     for delta in (1, 3, 0):
         for p in range(PARTS):
             near(p, delta).start()
+
+    with scope("barrier"):
+
+        @pl.when(core == 1)
+        def _():
+            pl.semaphore_wait(barrier, 12)
+            pl.semaphore_signal(pal, inc=1, device_id={"store": 0}, device_id_type=MESH)
+
+        @pl.when(core == 0)
+        def _():
+            pl.semaphore_wait(pal, 1)
+
+    for to in beside:
+        pl.semaphore_signal(ready, inc=1, device_id=to, device_id_type=MESH)
 
     def arrived(ref, sem, ssem=s1):
         copy(ref, ref, ssem, sem, partner).wait_recv()
@@ -333,8 +359,8 @@
                     c_own * d[p, 0, k, rows, :] + c_one * rb[way, p, k, rows, :] + c_two * rc[way, p, k, rows, :]
                 )
             e[p, k, 0:STAT, :] = factors[p, 0][1]
-            if turn[k]:
-                copy(e.at[p, k], r2.at[p, turn[k] - 1], s2, v2.at[p], peer(order[p][1], turn[k])).start()
+            to = across(order[p][1], turn[k])
+            copy(e.at[p, k], r2.at[p, turn[k]], s2, v2.at[p], to).start()
 
     issue(2)
     with scope("lm"):
@@ -361,17 +387,17 @@
     for p in range(PARTS):
         with scope("w2"):
             copy(r2.at[p], r2.at[p], s2, v2.at[p], partner).wait_recv()
-        scales, stats = combine([e[p, 3, 0:STAT, :]] + [r2[p, i, 0:STAT, :] for i in range(3)])
+        scales, stats = combine([r2[p, i, 0:STAT, :] for i in range(RING)])
         for c in range(RING):
             rows = slice(STAT + c * SLOTS, STAT + (c + 1) * SLOTS)
-            total = scales[0] * e[p, 3, rows, :]
-            for i in range(3):
-                total = total + scales[i + 1] * r2[p, i, rows, :]
+            total = scales[0] * r2[p, 0, rows, :]
+            for i in range(1, RING):
+                total = total + scales[i] * r2[p, i, rows, :]
             g3[p, c, 0:SLOTS, :] = total
             g3[p, c, SLOTS:MSG3, :] = stats[0 : MSG3 - SLOTS]
-        for delta in (2, 1, 3):
+        for delta in (2, 1, 3, 0):
             to = (last[p] + delta) % RING
-            copy(g3.at[p, to], r3.at[p, delta - 1], s3, v3.at[p], peer(order[p][2], delta)).start()
+            copy(g3.at[p, to], r3.at[p, delta], s3, v3.at[p], across(order[p][2], delta)).start()
 
     slots = logits.shape[1] // GROUPS
     mix = mix_ref[0, 0]
@@ -391,7 +417,7 @@
     for p in range(PARTS):
         with scope("w3"):
             copy(r3.at[p], r3.at[p], s3, v3.at[p], partner).wait_recv()
-        blocks = [g3[p, last[p]]] + [r3[p, i] for i in range(3)]
+        blocks = [r3[p, i] for i in range(RING)]
         scales, stats = combine([v[SLOTS : SLOTS + 2] for v in blocks])
         count = min(SLOTS, slots - p * SLOTS)
         total = sum(c * v[0:count] for c, v in zip(scales, blocks))
@@ -453,9 +479,9 @@
                 pltpu.VMEM((2, PARTS, RING, MSG2, LANES), F32),
                 pltpu.VMEM((2, PARTS, RING, MSG2, LANES), F32),
                 pltpu.VMEM((PARTS, RING, MSG2, LANES), F32),
-                pltpu.VMEM((PARTS, RING - 1, MSG2, LANES), F32),
+                pltpu.VMEM((PARTS, RING, MSG2, LANES), F32),
                 pltpu.VMEM((PARTS, RING, MSG3, LANES), F32),
-                pltpu.VMEM((PARTS, RING - 1, MSG3, LANES), F32),
+                pltpu.VMEM((PARTS, RING, MSG3, LANES), F32),
                 pltpu.VMEM((3, STAT, LANES), F32),
                 pltpu.VMEM((3, RING - 1, STAT, LANES), F32),
                 pltpu.VMEM((LANES, LANES), F32),
@@ -467,6 +493,7 @@
                 pltpu.SemaphoreType.DMA((4,)),
                 pltpu.SemaphoreType.DMA((12,)),
                 pltpu.SemaphoreType.REGULAR,
+                pltpu.SemaphoreType.REGULAR,
             ]
             + [pltpu.SemaphoreType.DMA, pltpu.SemaphoreType.DMA((3,))] * 3,
             compiler_params=pltpu.CompilerParams(collective_id=0, has_side_effects=True, vmem_limit_bytes=KB_LIMIT * 2**20),

time: 34.1 us -> 32.6 us (0.956); the launches traced: 33.5 us -> 32.3 us
  Pallas kernels: 31.5 us -> 30.4 us
    pallas_call x1, Pallas kernels: 23.1 us -> 22 us  [local_step(): pl.pallas_call(comm_kernel, out_shape=jax.ShapeDtypeStruct((ROWS, vocab_l...]
where the time goes in v8:
time: 32.6 us; the launch traced here: 32.3 us
  Pallas kernels  30.4 us (93%)
  between operations  1.33 us (4%)
  local copies, waits for them, and re-layouts  0.62 us (2%)
    pallas_call x1, Pallas kernels, local_step(): pl.pallas_call(comm_kernel, out_shape=jax.ShapeDtypeStruct((ROWS, vocab_l...  22 us
    pallas_call x1, Pallas kernels, local_step(): pl.pallas_call(functools.partial(local_kernel, vocab_loc), out_shape=[jax...  8.38 us

profile of v8, /device:TPU:1, one launch (start us, length us, event | category | flops | bytes accessed | tf_op | source)
XLA Modules:
  0.0 32.3 jit_solution(8651030372681067409)
XLA Ops:
  1.3 0.0 copy-start
  1.3 8.4 %histogram.1 = (f32[6928,128]{1,0:T(8,128)S(1)}, f32[6928,128]{1,0:T(8,128)S(1)}, f32[6928,128]{1,0:T(8,128)S(1)}, f32[6928,128]{1,0:T(8,128)S(1)}, f32[8,256]{1,0:T(8,128)S(1)}) custom-call(f32[1,1]{1,0:T(1,128)} %bitcast.4.tau_ref, s32[16,128]{1,0:T(8,128)} %bitcast.7, bf16[16,2560]{1,0:T(8,128)(2,1)} %q_ref.1, bf16[2048,2560]{1,0:T(8,128)(2,1)} %k_hbm.1), custom_call_target="tpu_custom_call" | custom-call | tf_op jit(solution)/shard_map/histogram/pallas_call | solution.py:442
  9.7 0.0 copy-done
  9.7 22.0 %exchange.1 = f32[8,800]{1,0:T(8,128)S(1)} custom-call(f32[1,1]{1,0:T(1,128)} %bitcast.5.mix_ref, f32[6928,128]{1,0:T(8,128)S(1)} %get-tuple-element.10.h0, f32[6928,128]{1,0:T(8,128)S(1)} %get-tuple-element.11.h1, f32[6928,128]{1,0:T(8,128)S(1)} %get-tuple-element.12.h2, f32[6928,128]{1,0:T(8,128)S(1)} %get-tuple-element.13.h3, ...), custom_call_target="tpu_custom_call" | custom-call | tf_op jit(solution)/shard_map/exchange/pallas_call | solution.py:466
  31.7 0.6 %copy.10 = f32[8,800]{1,0:T(8,128)} copy(f32[8,800]{1,0:T(8,128)S(1)} %exchange.1) | data formatting | bytes 51200
Async XLA Ops:
  1.3 8.4 %copy-start = (bf16[16,2560]{1,0:T(8,128)(2,1)S(1)}, bf16[16,2560]{1,0:T(8,128)(2,1)}, u32[]{:S(2)}) copy-start(bf16[16,2560]{1,0:T(8,128)(2,1)} %q_ref.1) | copy-start | bytes 245764

commit v9 on v8

--- a/solution.py
+++ b/solution.py
@@ -41,7 +41,7 @@
     n_keys = k_ref.shape[0]
     quarter = n_keys // NBUF
     chunk = quarter // 2
-    part_rows = 64
+    part_rows = 128
 
     def fetch(j):
         rows = pl.ds(pl.multiple_of(j * chunk, chunk), chunk)
@@ -144,7 +144,7 @@
             stats_ref[pl.ds(NBUF + b, 1), :] = total
 
     pltpu.make_async_copy(idx, tok_ref, isem).wait()
-    unroll = 8
+    unroll = 16
     rows = quarter // LANES
     with scope("scatter"):
         for c in range(rows):
@@ -363,6 +363,7 @@
             copy(e.at[p, k], r2.at[p, turn[k]], s2, v2.at[p], to).start()
 
     issue(2)
+    issue(1)
     with scope("lm"):
         head.wait()
         both = lax.dot_general(q_ref[...], w_ref[...], (((1,), (1,)), ((), ())), preferred_element_type=F32)
@@ -375,8 +376,8 @@
         pair = jnp.concatenate([pair] * GROUPS, axis=0).T
         pl.semaphore_wait(ready, 6)
         link(0, pair[0:8, :])
-    for delta in (1, 3, 0):
-        issue(delta)
+    issue(3)
+    issue(0)
     for b in range(RING):
         relay(b)
     link(1, unlink(0))

time: 32.6 us -> 32.3 us (level)
  no operation moved by 1% of the time
where the time goes in v9:
time: 32.3 us; the launch traced here: 32.2 us
  Pallas kernels  30.2 us (93%)
  between operations  1.33 us (4%)
  local copies, waits for them, and re-layouts  0.62 us (2%)
    pallas_call x1, Pallas kernels, local_step(): pl.pallas_call(comm_kernel, out_shape=jax.ShapeDtypeStruct((ROWS, vocab_l...  22 us
    pallas_call x1, Pallas kernels, local_step(): pl.pallas_call(functools.partial(local_kernel, vocab_loc), out_shape=[jax...  8.27 us

profile of v9, /device:TPU:1, one launch (start us, length us, event | category | flops | bytes accessed | tf_op | source)
XLA Modules:
  0.0 32.2 jit_solution(567607523638364768)
XLA Ops:
  1.3 0.0 copy-start
  1.3 8.3 %histogram.1 = (f32[6928,128]{1,0:T(8,128)S(1)}, f32[6928,128]{1,0:T(8,128)S(1)}, f32[6928,128]{1,0:T(8,128)S(1)}, f32[6928,128]{1,0:T(8,128)S(1)}, f32[8,256]{1,0:T(8,128)S(1)}) custom-call(f32[1,1]{1,0:T(1,128)} %bitcast.4.tau_ref, s32[16,128]{1,0:T(8,128)} %bitcast.7, bf16[16,2560]{1,0:T(8,128)(2,1)} %q_ref.1, bf16[2048,2560]{1,0:T(8,128)(2,1)} %k_hbm.1), custom_call_target="tpu_custom_call" | custom-call | tf_op jit(solution)/shard_map/histogram/pallas_call | solution.py:443
  9.6 0.0 copy-done
  9.6 22.0 %exchange.1 = f32[8,800]{1,0:T(8,128)S(1)} custom-call(f32[1,1]{1,0:T(1,128)} %bitcast.5.mix_ref, f32[6928,128]{1,0:T(8,128)S(1)} %get-tuple-element.10.h0, f32[6928,128]{1,0:T(8,128)S(1)} %get-tuple-element.11.h1, f32[6928,128]{1,0:T(8,128)S(1)} %get-tuple-element.12.h2, f32[6928,128]{1,0:T(8,128)S(1)} %get-tuple-element.13.h3, ...), custom_call_target="tpu_custom_call" | custom-call | tf_op jit(solution)/shard_map/exchange/pallas_call | solution.py:467
  31.6 0.6 %copy.10 = f32[8,800]{1,0:T(8,128)} copy(f32[8,800]{1,0:T(8,128)S(1)} %exchange.1) | data formatting | bytes 51200
Async XLA Ops:
  1.3 8.3 %copy-start = (bf16[16,2560]{1,0:T(8,128)(2,1)S(1)}, bf16[16,2560]{1,0:T(8,128)(2,1)}, u32[]{:S(2)}) copy-start(bf16[16,2560]{1,0:T(8,128)(2,1)} %q_ref.1) | copy-start | bytes 245764

commit v10 on v9

--- a/solution.py
+++ b/solution.py
@@ -104,7 +104,9 @@
             for g in range(GROUPS // 2):
                 qrep[pl.ds(h * LANES + g * 2 * ROWS, 2 * ROWS), :] = pair
 
-    inv = 1.0 / tau_ref[0, 0]
+    tau = tau_ref[0, 0]
+    unit = jnp.where(tau > 1.0, 2.0**-64, 1.0)
+    inv = 1.0 / (tau * unit)
     lane_group = (lax.broadcasted_iota(jnp.int32, (LANES, LANES), 1) // ROWS).astype(F32)
 
     @pl.loop(0, NBUF)
@@ -122,7 +124,7 @@
                     kf = keys[r : r + part_rows, c : c + LANES].astype(F32)
                     squares = squares + kf * kf
                 norms = jnp.sum(squares, axis=1, keepdims=True)
-                scores = (2.0 * dots[r : r + part_rows] - norms) * inv
+                scores = ((2.0 * unit) * dots[r : r + part_rows] - unit * norms) * inv
                 sc[r : r + part_rows, :] = scores
                 tops.append(jnp.max(scores.reshape(part_rows // 8, 8, 2 * LANES), axis=0))
             m = jnp.max(functools.reduce(jnp.maximum, tops), axis=0, keepdims=True)
@@ -218,13 +220,6 @@
                     row = t * 8 if t * 8 < LEAD else t * 8 + STAT
                     loc[h, blk, b, row : row + 8, :] = total
 
-    with scope("sum"):
-        pl.loop(0, PARTS)(add_up)
-
-    @pl.when(core == 1)
-    def _():
-        pl.semaphore_wait(pal, 1)
-
     def copy(src, dst, ssem, rsem, to):
         return pltpu.make_async_remote_copy(src_ref=src, dst_ref=dst, send_sem=ssem, recv_sem=rsem, device_id=to, device_id_type=MESH)
 
@@ -255,11 +250,22 @@
         blk = place(p, delta)
         return copy(loc.at[1 - core, blk], din.at[blk], s0, v0.at[p if delta == 2 else NEAR[delta]], partner)
 
-    for p in range(PARTS):
-        near(p, 2).start()
+    with scope("sum"):
+
+        @pl.loop(0, PARTS)
+        def _(p):
+            add_up(p)
+
+            @pl.when(jnp.logical_and(core == 1, p == 0))
+            def _():
+                pl.semaphore_wait(pal, 1)
+
+            blk = p * RING + ((chip >> (2 * p)) + 2) % RING
+            copy(loc.at[1 - core, blk], din.at[blk], s0, v0.at[p], partner).start()
+
     with scope("sum2"):
-        pl.loop(PARTS, PARTS * RING)(add_up)
-    for delta in (1, 3, 0):
+        pl.loop(PARTS, 3 * PARTS)(add_up)
+    for delta in (1, 3):
         for p in range(PARTS):
             near(p, delta).start()
 
@@ -309,7 +315,7 @@
                 elif p == 0:
                     arrived(din.at[0:PARTS], v0.at[NEAR[delta]], s0)
             if not chipwise:
-                chipwise.append(combine([loc[core, 0, 0, tile, :], din[blk, 0, tile, :]]))
+                chipwise.append(combine([loc[core, blk, 0, tile, :], din[blk, 0, tile, :]]))
             (c_own, c_par), stats = chipwise[0]
             for k in range(RING):
                 b = (mid[p] + turn[k]) % RING
@@ -363,6 +369,10 @@
             copy(e.at[p, k], r2.at[p, turn[k]], s2, v2.at[p], to).start()
 
     issue(2)
+    with scope("sum3"):
+        pl.loop(3 * PARTS, 4 * PARTS)(add_up)
+    for p in range(PARTS):
+        near(p, 0).start()
     issue(1)
     with scope("lm"):
         head.wait()

time: 32.3 us -> 32.2 us (level)
  no operation moved by 1% of the time
where the time goes in v10:
time: 32.2 us; the launch traced here: 32.1 us
  Pallas kernels  30.2 us (94%)
  between operations  1.33 us (4%)
  local copies, waits for them, and re-layouts  0.62 us (2%)
    pallas_call x1, Pallas kernels, local_step(): pl.pallas_call(comm_kernel, out_shape=jax.ShapeDtypeStruct((ROWS, vocab_l...  21.8 us
    pallas_call x1, Pallas kernels, local_step(): pl.pallas_call(functools.partial(local_kernel, vocab_loc), out_shape=[jax...  8.33 us

profile of v10, /device:TPU:1, one launch (start us, length us, event | category | flops | bytes accessed | tf_op | source)
XLA Modules:
  0.0 32.1 jit_solution(7402218385291630464)
XLA Ops:
  1.3 0.0 copy-start
  1.3 8.3 %histogram.1 = (f32[6928,128]{1,0:T(8,128)S(1)}, f32[6928,128]{1,0:T(8,128)S(1)}, f32[6928,128]{1,0:T(8,128)S(1)}, f32[6928,128]{1,0:T(8,128)S(1)}, f32[8,256]{1,0:T(8,128)S(1)}) custom-call(f32[1,1]{1,0:T(1,128)} %bitcast.4.tau_ref, s32[16,128]{1,0:T(8,128)} %bitcast.7, bf16[16,2560]{1,0:T(8,128)(2,1)} %q_ref.1, bf16[2048,2560]{1,0:T(8,128)(2,1)} %k_hbm.1), custom_call_target="tpu_custom_call" | custom-call | tf_op jit(solution)/shard_map/histogram/pallas_call | solution.py:453
  9.6 0.0 copy-done
  9.7 21.8 %exchange.1 = f32[8,800]{1,0:T(8,128)S(1)} custom-call(f32[1,1]{1,0:T(1,128)} %bitcast.5.mix_ref, f32[6928,128]{1,0:T(8,128)S(1)} %get-tuple-element.10.h0, f32[6928,128]{1,0:T(8,128)S(1)} %get-tuple-element.11.h1, f32[6928,128]{1,0:T(8,128)S(1)} %get-tuple-element.12.h2, f32[6928,128]{1,0:T(8,128)S(1)} %get-tuple-element.13.h3, ...), custom_call_target="tpu_custom_call" | custom-call | tf_op jit(solution)/shard_map/exchange/pallas_call | solution.py:477
  31.5 0.6 %copy.10 = f32[8,800]{1,0:T(8,128)} copy(f32[8,800]{1,0:T(8,128)S(1)} %exchange.1) | data formatting | bytes 51200
Async XLA Ops:
  1.3 8.4 %copy-start = (bf16[16,2560]{1,0:T(8,128)(2,1)S(1)}, bf16[16,2560]{1,0:T(8,128)(2,1)}, u32[]{:S(2)}) copy-start(bf16[16,2560]{1,0:T(8,128)(2,1)} %q_ref.1) | copy-start | bytes 245764

commit v11 on v10

--- a/solution.py
+++ b/solution.py
@@ -146,7 +146,7 @@
             stats_ref[pl.ds(NBUF + b, 1), :] = total
 
     pltpu.make_async_copy(idx, tok_ref, isem).wait()
-    unroll = 16
+    unroll = 32
     rows = quarter // LANES
     with scope("scatter"):
         for c in range(rows):

time: 32.2 us -> 32.2 us (level)
  no operation moved by 1% of the time
where the time goes in v11:
time: 32.2 us; the launch traced here: 32.1 us
  Pallas kernels  30.1 us (93%)
  between operations  1.33 us (4%)
  local copies, waits for them, and re-layouts  0.62 us (2%)
    pallas_call x1, Pallas kernels, local_step(): pl.pallas_call(comm_kernel, out_shape=jax.ShapeDtypeStruct((ROWS, vocab_l...  21.8 us
    pallas_call x1, Pallas kernels, local_step(): pl.pallas_call(functools.partial(local_kernel, vocab_loc), out_shape=[jax...  8.3 us

profile of v11, /device:TPU:1, one launch (start us, length us, event | category | flops | bytes accessed | tf_op | source)
XLA Modules:
  0.0 32.1 jit_solution(764390638104334442)
XLA Ops:
  1.3 0.0 copy-start
  1.3 8.3 %histogram.1 = (f32[6928,128]{1,0:T(8,128)S(1)}, f32[6928,128]{1,0:T(8,128)S(1)}, f32[6928,128]{1,0:T(8,128)S(1)}, f32[6928,128]{1,0:T(8,128)S(1)}, f32[8,256]{1,0:T(8,128)S(1)}) custom-call(f32[1,1]{1,0:T(1,128)} %bitcast.4.tau_ref, s32[16,128]{1,0:T(8,128)} %bitcast.7, bf16[16,2560]{1,0:T(8,128)(2,1)} %q_ref.1, bf16[2048,2560]{1,0:T(8,128)(2,1)} %k_hbm.1), custom_call_target="tpu_custom_call" | custom-call | tf_op jit(solution)/shard_map/histogram/pallas_call | solution.py:453
  9.6 0.0 copy-done
  9.6 21.8 %exchange.1 = f32[8,800]{1,0:T(8,128)S(1)} custom-call(f32[1,1]{1,0:T(1,128)} %bitcast.5.mix_ref, f32[6928,128]{1,0:T(8,128)S(1)} %get-tuple-element.10.h0, f32[6928,128]{1,0:T(8,128)S(1)} %get-tuple-element.11.h1, f32[6928,128]{1,0:T(8,128)S(1)} %get-tuple-element.12.h2, f32[6928,128]{1,0:T(8,128)S(1)} %get-tuple-element.13.h3, ...), custom_call_target="tpu_custom_call" | custom-call | tf_op jit(solution)/shard_map/exchange/pallas_call | solution.py:477
  31.5 0.6 %copy.10 = f32[8,800]{1,0:T(8,128)} copy(f32[8,800]{1,0:T(8,128)S(1)} %exchange.1) | data formatting | bytes 51200
Async XLA Ops:
  1.3 8.3 %copy-start = (bf16[16,2560]{1,0:T(8,128)(2,1)S(1)}, bf16[16,2560]{1,0:T(8,128)(2,1)}, u32[]{:S(2)}) copy-start(bf16[16,2560]{1,0:T(8,128)(2,1)} %q_ref.1) | copy-start | bytes 245764

commit v12 on v11

--- a/solution.py
+++ b/solution.py
@@ -41,7 +41,7 @@
     n_keys = k_ref.shape[0]
     quarter = n_keys // NBUF
     chunk = quarter // 2
-    part_rows = 128
+    part_rows = 256
 
     def fetch(j):
         rows = pl.ds(pl.multiple_of(j * chunk, chunk), chunk)

time: 32.2 us -> 32.2 us (level)
  no operation moved by 1% of the time
where the time goes in v12:
time: 32.2 us; the launch traced here: 32 us
  Pallas kernels  30.1 us (93%)
  between operations  1.33 us (4%)
  local copies, waits for them, and re-layouts  0.62 us (2%)
    pallas_call x1, Pallas kernels, local_step(): pl.pallas_call(comm_kernel, out_shape=jax.ShapeDtypeStruct((ROWS, vocab_l...  21.8 us
    pallas_call x1, Pallas kernels, local_step(): pl.pallas_call(functools.partial(local_kernel, vocab_loc), out_shape=[jax...  8.26 us

profile of v12, /device:TPU:1, one launch (start us, length us, event | category | flops | bytes accessed | tf_op | source)
XLA Modules:
  0.0 32.0 jit_solution(14321927794620402347)
XLA Ops:
  1.3 0.0 copy-start
  1.3 8.3 %histogram.1 = (f32[6928,128]{1,0:T(8,128)S(1)}, f32[6928,128]{1,0:T(8,128)S(1)}, f32[6928,128]{1,0:T(8,128)S(1)}, f32[6928,128]{1,0:T(8,128)S(1)}, f32[8,256]{1,0:T(8,128)S(1)}) custom-call(f32[1,1]{1,0:T(1,128)} %bitcast.4.tau_ref, s32[16,128]{1,0:T(8,128)} %bitcast.7, bf16[16,2560]{1,0:T(8,128)(2,1)} %q_ref.1, bf16[2048,2560]{1,0:T(8,128)(2,1)} %k_hbm.1), custom_call_target="tpu_custom_call" | custom-call | tf_op jit(solution)/shard_map/histogram/pallas_call | solution.py:453
  9.6 0.0 copy-done
  9.6 21.8 %exchange.1 = f32[8,800]{1,0:T(8,128)S(1)} custom-call(f32[1,1]{1,0:T(1,128)} %bitcast.5.mix_ref, f32[6928,128]{1,0:T(8,128)S(1)} %get-tuple-element.10.h0, f32[6928,128]{1,0:T(8,128)S(1)} %get-tuple-element.11.h1, f32[6928,128]{1,0:T(8,128)S(1)} %get-tuple-element.12.h2, f32[6928,128]{1,0:T(8,128)S(1)} %get-tuple-element.13.h3, ...), custom_call_target="tpu_custom_call" | custom-call | tf_op jit(solution)/shard_map/exchange/pallas_call | solution.py:477
  31.4 0.6 %copy.10 = f32[8,800]{1,0:T(8,128)} copy(f32[8,800]{1,0:T(8,128)S(1)} %exchange.1) | data formatting | bytes 51200
Async XLA Ops:
  1.3 8.3 %copy-start = (bf16[16,2560]{1,0:T(8,128)(2,1)S(1)}, bf16[16,2560]{1,0:T(8,128)(2,1)}, u32[]{:S(2)}) copy-start(bf16[16,2560]{1,0:T(8,128)(2,1)} %q_ref.1) | copy-start | bytes 245764
